TPU v7x, 256 devices: a whole 4x4x8 slice. The times are simulated.
256 devices in a mesh: node: 64 (over z, y_lo, x), expert: 4 (over y_hi, core).
Axes of the slice: x: 4, y: 4 (y_hi: 2, y_lo: 2; y = y_hi * 2 + y_lo), z: 8, core: 2. Of those that a mesh axis runs over, the one named last changes fastest.
Arguments:
- param_gu: float32 [262144, 1024], P('node', 'expert'), may hold values from -13 to 13
- param_down: float32 [8192, 16384], P('node', 'expert'), may hold values from -13 to 13
- tokens: bfloat16 [32768, 4096], P(('node', 'expert')), may hold values from -6 to 6
- cotangent: bfloat16 [32768, 4096], P(('node', 'expert')), may hold values from -6 to 6
- routes: int32 [32768, 2], P(('node', 'expert')), may hold values from 0 to 3, all different within a row; in each aligned block of 128 rows (0 to 127, 128 to 255, ...) at most 96 rows name the same one
- plan: int32 [4], replicated, may hold values from 0 to 5
Outputs:
- gossiped_gu: bfloat16 [262144, 1024], P('node', 'expert')
- gossiped_down: bfloat16 [8192, 16384], P('node', 'expert')
- averaged_gu: float32 [4096, 1024], P('node', 'expert')
- averaged_down: float32 [128, 16384], P('node', 'expert')
Inputs may be any that keep to these rules, and one draw needn't show every extreme that they name: `routes`: each row names 2 different experts; the rows of one device name one expert 96 times at most.
All inputs are finite; a program needn't handle non-finite values.
Results may differ from a plain program's by a relative error of at most 0.0078.
Values may be sent and summed in bfloat16 or wider, within the bound.
A program may use at most 128 MiB of HBM per device.

v0:
```python
import math

import jax
import jax.numpy as jnp
from jax import lax
from jax.experimental import pallas as pl
from jax.experimental.pallas import tpu as pltpu
from jax.sharding import PartitionSpec as P

MESH = pl.DeviceIdType.MESH
ROUNDS = 4
CHUNKS = 3


def expert_step(x, dy, picked, param_gu, param_down):
    hid, width = param_down.shape
    wgu = param_gu.astype(jnp.bfloat16)
    wdown = param_down.astype(jnp.bfloat16)
    both = jnp.dot(x, wgu, preferred_element_type=jnp.float32) * (1.0 / math.sqrt(width))
    gate = both[:, :hid]
    upper = both[:, hid:]
    sigma = jax.nn.sigmoid(gate)
    zero = jnp.zeros((), jnp.float32)
    act = jnp.where(picked, gate * sigma * upper, zero).astype(jnp.bfloat16)
    dact = lax.dot_general(
        dy, wdown, (((1,), (1,)), ((), ())), preferred_element_type=jnp.float32
    ) * (1.0 / math.sqrt(hid))
    dgate = dact * upper * sigma * (1.0 + gate * (1.0 - sigma))
    dupper = dact * gate * sigma
    dboth = jnp.where(picked, jnp.concatenate([dgate, dupper], axis=1), zero).astype(jnp.bfloat16)
    grad_down = lax.dot_general(
        act, dy, (((0,), (0,)), ((), ())), preferred_element_type=jnp.float32
    ) * (1.0 / math.sqrt(hid))
    grad_gu = lax.dot_general(
        x, dboth, (((0,), (0,)), ((), ())), preferred_element_type=jnp.float32
    ) * (1.0 / math.sqrt(width))
    return param_gu - 0.5 * grad_gu, param_down - 0.5 * grad_down


def gossip_kernel(
    nodes, zs, ys, xs, shifts, src, out, mean, half, done, send1, recv1, send2, recv2, keep, *gots
):
    me = lax.axis_index("node")
    rows = src.shape[1] // CHUNKS
    z, y, x = me // (ys * xs), (me // xs) % ys, me % xs

    def peer_at(t):
        j, k = t % zs, t // zs
        dz = (j % 2) * ((j + 1) // 2) + (1 - j % 2) * (zs - j // 2)
        dy, dx = k // xs, k % xs
        return ((z + dz) % zs) * (ys * xs) + ((y + dy) % ys) * xs + (x + dx) % xs

    barrier = pltpu.get_barrier_semaphore()

    @pl.loop(1, nodes)
    def _(t):
        pl.semaphore_signal(barrier, inc=1, device_id={"node": peer_at(t)}, device_id_type=MESH)

    pl.semaphore_wait(barrier, nodes - 1)

    def part(ref, index, c):
        return ref.at[index, pl.ds(c * rows, rows)]

    def first(t, c):
        peer = peer_at(t)
        return pltpu.make_async_remote_copy(
            src_ref=part(src, peer, c),
            dst_ref=gots[c].at[me],
            send_sem=send1.at[c],
            recv_sem=recv1.at[c],
            device_id={"node": peer},
            device_id_type=MESH,
        )

    def second(t, c):
        peer = peer_at(t)
        return pltpu.make_async_remote_copy(
            src_ref=part(done, peer, c),
            dst_ref=part(out, me, c),
            send_sem=send2.at[c],
            recv_sem=recv2.at[c],
            device_id={"node": peer},
            device_id_type=MESH,
        )

    def all_of(c, send, recv):
        most = gots[c].at[pl.ds(0, nodes - 1)]
        return pltpu.make_async_remote_copy(
            src_ref=most,
            dst_ref=most,
            send_sem=send.at[c],
            recv_sem=recv.at[c],
            device_id={"node": (me + 1) % nodes},
            device_id_type=MESH,
        )

    for c in range(CHUNKS):

        @pl.loop(1, nodes)
        def _(t):
            first(t, c).start()

        gots[c][me] = src[me, pl.ds(c * rows, rows)]

    for c in range(CHUNKS):
        span = pl.ds(c * rows, rows)
        all_of(c, send1, recv1).wait_recv()
        s0, s1, s2, s3 = shifts[0], shifts[1], shifts[2], shifts[3]

        def wide(index):
            return gots[c][lax.rem(index, nodes)].astype(jnp.float32)

        def early(n, total):
            own = wide(n)
            half[n] = (own + wide(n + s0)) + (wide(n + s1) + wide(n + s0 + s1))
            return total + own

        total = lax.fori_loop(0, nodes, early, jnp.zeros(half.shape[1:], jnp.float32))
        mean[span] = total * (1.0 / nodes)

        def late(n, carry):
            value = (half[n] + half[lax.rem(n + s2, nodes)]) + (
                half[lax.rem(n + s3, nodes)] + half[lax.rem(n + s2 + s3, nodes)]
            )
            done[n, span] = (value * (1.0 / 16.0)).astype(done.dtype)
            return carry

        lax.fori_loop(0, nodes, late, 0)

        @pl.loop(1, nodes)
        def _(t):
            second(t, c).start()

        pltpu.make_async_copy(part(done, me, c), part(out, me, c), keep.at[c]).start()

    for c in range(CHUNKS):
        all_of(c, send1, recv1).wait_send()
        all_of(c, send2, recv2).wait_send()
        all_of(c, send2, recv2).wait_recv()
        pltpu.make_async_copy(part(done, me, c), part(out, me, c), keep.at[c]).wait()


def gossip(packed, shifts, nodes):
    _, rows, lanes = packed.shape
    ys, xs = 2, 4
    zs = nodes // (ys * xs)

    def body(*refs):
        gossip_kernel(nodes, zs, ys, xs, *refs)

    return pl.pallas_call(
        body,
        out_shape=(
            jax.ShapeDtypeStruct(packed.shape, jnp.bfloat16),
            jax.ShapeDtypeStruct((rows, lanes), jnp.float32),
        ),
        in_specs=[
            pl.BlockSpec(memory_space=pltpu.SMEM),
            pl.BlockSpec(memory_space=pltpu.VMEM),
        ],
        out_specs=(
            pl.BlockSpec(memory_space=pl.ANY),
            pl.BlockSpec(memory_space=pltpu.VMEM),
        ),
        scratch_shapes=[
            pltpu.VMEM((nodes, rows // CHUNKS, lanes), jnp.float32),
            pltpu.VMEM(packed.shape, jnp.bfloat16),
            pltpu.SemaphoreType.DMA((CHUNKS,)),
            pltpu.SemaphoreType.DMA((CHUNKS,)),
            pltpu.SemaphoreType.DMA((CHUNKS,)),
            pltpu.SemaphoreType.DMA((CHUNKS,)),
            pltpu.SemaphoreType.DMA((CHUNKS,)),
        ]
        + [pltpu.VMEM((nodes, rows // CHUNKS, lanes), jnp.bfloat16)] * CHUNKS,
        compiler_params=pltpu.CompilerParams(
            collective_id=1, has_side_effects=True, vmem_limit_bytes=32 * 1024 * 1024
        ),
        name="gossip",
    )(shifts, packed)


def step(param_gu, param_down, tokens, cotangent, routes, plan):
    nodes = lax.axis_size("node")
    expert = lax.axis_index("expert")
    width, cols = param_gu.shape
    hid = param_down.shape[0]
    x = lax.all_gather(tokens, "expert", axis=0, tiled=True)
    dy = lax.all_gather(cotangent, "expert", axis=0, tiled=True)
    named = lax.all_gather(routes, "expert", axis=0, tiled=True)
    picked = jnp.any(named == expert, axis=1)[:, None]
    new_gu, new_down = expert_step(x, dy, picked, param_gu, param_down)
    own_gu, own_down = width // nodes, hid // nodes
    lanes = cols
    packed = jnp.concatenate(
        [
            new_gu.astype(jnp.bfloat16).reshape(nodes, own_gu, lanes),
            new_down.astype(jnp.bfloat16).reshape(nodes, own_down * width // lanes, lanes),
        ],
        axis=1,
    )
    shifts = jnp.left_shift(jnp.int32(1), plan)
    mixed, mean = gossip(packed, shifts, nodes)
    gossiped_gu = mixed[:, :own_gu].reshape(width, cols)
    gossiped_down = mixed[:, own_gu:].reshape(hid, width)
    averaged_gu = mean[:own_gu]
    averaged_down = mean[own_gu:].reshape(own_down, width)
    return gossiped_gu, gossiped_down, averaged_gu, averaged_down


def solution(mesh):
    both = P(("node", "expert"), None)
    split = P("node", "expert")
    return jax.shard_map(
        step,
        mesh=mesh,
        in_specs=(split, split, both, both, both, P()),
        out_specs=(split, split, split, split),
        check_vma=False,
    )
```

profile of v0, /device:TPU:1, one launch (start us, length us, event | category | flops | bytes accessed | tf_op | source)
XLA Modules:
  0.0 273.7 jit_solution(2156176154871469087)
XLA Ops:
  7.2 0.0 all-gather.5.cloned.1.call-start
  7.2 0.7 all-gather.5.cloned.1.call-update
  7.9 0.0 all-gather.3.cloned.1.call-start
  7.9 0.7 all-gather.3.cloned.1.call-update
  8.7 0.0 copy-start.3
  8.7 0.0 copy-start.4
  8.7 5.7 %copy.10 = f32[4096,256]{0,1:T(8,128)} copy(f32[4096,256]{1,0:T(8,128)} %param.6) | data formatting | bytes 8388608 | tf_op args[0]
  14.4 0.0 copy-done.3
  14.4 9.6 %all_gather.9 = s32[512,2]{0,1:T(2,128)S(1)} all-gather(s32[128,2]{0,1:T(2,128)S(1)} %copy-done.3), channel_id=1, replica_groups=mesh['node'=64,'expert'=4] {'expert'}, dimensions={0}, use_global_device_ids=true | all-gather | bytes 5120 | tf_op jit(solution)/shard_map/all_gather | solution.py:189
  24.0 0.0 copy-done.4
  24.0 0.0 copy-start.1
  24.0 31.1 %all-gather.5.cloned.1.call-done = bf16[512,4096]{1,0:T(8,128)(2,1)} async-done(((bf16[128,4096]{1,0:T(8,128)(2,1)}), bf16[512,4096]{1,0:T(8,128)(2,1)}) %all-gather.5.cloned.1.call-update) | async-done | bytes 4194320 | tf_op jit(solution)/shard_map/all_gather | solution.py:187
  55.1 4.8 %fusion.7 = f32[512,256]{0,1:T(8,128)S(1)} fusion(bf16[512,4096]{1,0:T(8,128)(2,1)} %all-gather.5.cloned.1.call-done, f32[4096,256]{1,0:T(8,128)} %param.6), kind=kOutput, calls=%fused_computation.10 | convolution fusion | flops 1074921472 | bytes 8912896 | tf_op jit(solution)/shard_map/dot_general | solution.py:19
  59.8 0.0 copy-start.2
  59.9 37.6 %all-gather.3.cloned.1.call-done = bf16[512,4096]{1,0:T(8,128)(2,1)} async-done(((bf16[128,4096]{1,0:T(8,128)(2,1)}), bf16[512,4096]{1,0:T(8,128)(2,1)}) %all-gather.3.cloned.1.call-update) | async-done | bytes 4194320 | tf_op jit(solution)/shard_map/all_gather | solution.py:188
  97.4 0.0 copy-done.2
  97.4 0.0 copy-done.1
  97.4 4.0 %fusion.4 = bf16[128,4096]{1,0:T(8,128)(2,1)} fusion(f32[128,4096]{1,0:T(8,128)S(1)} %copy-done.1, bf16[512,4096]{1,0:T(8,128)(2,1)} %all-gather.3.cloned.1.call-done, f32[512,256]{0,1:T(8,128)S(1)} %fusion.7, pred[512]{0:T(512)(128)(4,1)S(1)} %compare_reduce_fusion), kind=kOutput, calls=%fused_computation.6 | convolution fusion | flops 538902528 | bytes 7864832 | tf_op jit(solution)/shard_map/dot_general | solution.py:31
  101.4 1.6 reshape.25
  103.0 0.0 copy-start
  103.0 4.0 %add_multiply_fusion = (bf16[512,128]{0,1:T(8,128)(2,1)S(1)}, bf16[512,128]{0,1:T(8,128)(2,1)S(1)}) fusion(f32[512,256]{0,1:T(8,128)} %copy-done.2, bf16[512,4096]{1,0:T(8,128)(2,1)} %all-gather.3.cloned.1.call-done, f32[128,4096]{1,0:T(8,128)S(1)} %copy-done.1), kind=kOutput, calls=%fused_computation.18 | convolution fusion | flops 538312704 | bytes 7077888 | tf_op jit(solution)/shard_map/dot_general | solution.py:25
  107.0 0.0 copy-done
  107.0 4.8 %fusion.2 = bf16[4096,256]{0,1:T(8,128)(2,1)} fusion(f32[4096,256]{0,1:T(8,128)S(1)} %copy-done, bf16[512,4096]{1,0:T(8,128)(2,1)} %all-gather.5.cloned.1.call-done, bf16[512,128]{0,1:T(8,128)(2,1)S(1)} %get-tuple-element.9, bf16[512,128]{0,1:T(8,128)(2,1)S(1)} %get-tuple-element.8, pred[512]{0:T(512)(128)(4,1)S(1)} %compare_reduce_fusion), kind=kOutput, calls=%fused_computation.3 | convolution fusion | flops 1077542912 | bytes 10748416 | tf_op jit(solution)/shard_map/dot_general | solution.py:34
  111.8 3.3 %copy.11 = bf16[4096,256]{1,0:T(8,128)(2,1)S(1)} copy(bf16[4096,256]{0,1:T(8,128)(2,1)} %fusion.2) | data formatting | bytes 4194304 | tf_op jit(solution)/shard_map/convert_element_type | solution.py:196
  115.1 0.3 pad_maximum_fusion.refs_1_
  115.4 147.3 %gossip.1 = (bf16[64,96,256]{2,1,0:T(8,128)(2,1)S(1)}, f32[96,256]{1,0:T(8,128)S(1)}) custom-call(s32[4]{0:T(128)S(1)} %broadcast_shift-left_fusion.refs_0_, bf16[64,96,256]{2,1,0:T(8,128)(2,1)S(1)} %pad_maximum_fusion.refs_1_), custom_call_target="tpu_custom_call" | custom-call | tf_op jit(solution)/shard_map/gossip/pallas_call | solution.py:151
  262.7 0.6 slice.22
  263.4 0.1 slice.21
  263.4 1.5 slice.20
  264.9 0.6 reshape.28
  265.6 1.3 reshape.27
  (3 shorter events, 0.0 us)
Async XLA Ops:
  7.2 47.9 %all-gather.5.cloned.1.call-start = ((), (), s32[]{:S(2)}) async-start(), calls=%async_computation.1 | async-start | bytes 5242880 | tf_op jit(solution)/shard_map/all_gather | solution.py:187
  7.9 89.5 %all-gather.3.cloned.1.call-start = ((), (), s32[]{:S(2)}) async-start(), calls=%async_computation | async-start | bytes 5242880 | tf_op jit(solution)/shard_map/all_gather | solution.py:188
  8.7 5.7 %copy-start.3 = (s32[128,2]{0,1:T(2,128)S(1)}, s32[128,2]{0,1:T(2,128)}, u32[]{:S(2)}) copy-start(s32[128,2]{0,1:T(2,128)} %param.10) | copy-start | bytes 3076
  8.7 15.3 %copy-start.4 = (s32[4]{0:T(128)S(1)}, s32[4]{0:T(128)}, u32[]{:S(2)}) copy-start(s32[4]{0:T(128)} %param.11) | copy-start | bytes 52
  24.0 73.4 %copy-start.1 = (f32[128,4096]{1,0:T(8,128)S(1)}, f32[128,4096]{1,0:T(8,128)}, u32[]{:S(2)}) copy-start(f32[128,4096]{1,0:T(8,128)} %param.7) | copy-start | bytes 6291460
  59.8 37.6 %copy-start.2 = (f32[512,256]{0,1:T(8,128)}, f32[512,256]{0,1:T(8,128)S(1)}, u32[]{:S(2)}) copy-start(f32[512,256]{0,1:T(8,128)S(1)} %fusion.7) | copy-start | bytes 1572868
  103.0 4.1 %copy-start = (f32[4096,256]{0,1:T(8,128)S(1)}, f32[4096,256]{0,1:T(8,128)}, u32[]{:S(2)}) copy-start(f32[4096,256]{0,1:T(8,128)} %copy.10) | copy-start | bytes 12582916
Sparse Core Ops, SparseCore 0:
  9.8 45.2 all-gather.4
  56.9 40.4 all-gather.2
where the time goes:
time: 274 us
  Pallas kernels  147 us (54%)
  waiting for transfers between devices  70 us (26%)
  matrix products  17.6 us (6%)
  local copies, waits for them, and re-layouts  14.7 us (5%)
  between operations  14.2 us (5%)
  blocking collectives  9.59 us (4%)
    pallas_call x1, Pallas kernels, gossip(): pl.pallas_call(body, out_shape=(jax.ShapeDtypeStruct(packed.shape, jnp.bf...  147 us
    all_gather x1, waiting for transfers between devices, step(): dy = lax.all_gather(cotangent, 'expert', axis=0, tiled=True)  37.6 us
    all_gather x1, waiting for transfers between devices, step(): x = lax.all_gather(tokens, 'expert', axis=0, tiled=True)  31.1 us
    all_gather x1, blocking collectives, step(): named = lax.all_gather(routes, 'expert', axis=0, tiled=True)  9.59 us
    unnamed x11, local copies, waits for them, and re-layouts  5.72 us
  transfers between devices with their start and end apart: 2, of which 2 were waited for; matrix products, arithmetic and copies ran while one was open for 4% of the time, Pallas kernels for 0%

commit v1 on v0

v1 whole, which is shorter than its diff:
```python
import math

import jax
import jax.numpy as jnp
from jax import lax
from jax.experimental import pallas as pl
from jax.experimental.pallas import tpu as pltpu
from jax.sharding import PartitionSpec as P

MESH = pl.DeviceIdType.MESH
X_PARTS = 2
DY_PARTS = 4
GU_PARTS = 4
LANES = 128
TILE = 512
Y_LO, X_SIZE = 2, 4


def kernel_body(
    nodes,
    shifts,
    code,
    tokens,
    cotangent,
    param_gu,
    param_down,
    out_gu,
    out_down,
    mean_gu,
    mean_down,
    x_all,
    dy_all,
    x_turned,
    gu_wide,
    down_wide,
    gu_short,
    down_short,
    both,
    dact,
    act_turned,
    dboth,
    codes,
    stage,
    half_gu,
    half_down,
    send_gu,
    send_down,
    done_gu,
    done_down,
    local_sem,
    block_sem,
    tok_send,
    tok_recv,
    gu_sem,
    down_sem,
    keep_gu,
    keep_down,
    *landing,
):
    got_gu, got_down = landing[:GU_PARTS], landing[GU_PARTS:]
    me = lax.axis_index("node")
    expert = lax.axis_index("expert")
    experts = lax.axis_size("expert")
    plane = Y_LO * X_SIZE
    zs = nodes // plane
    z, y, x = me // plane, (me // X_SIZE) % Y_LO, me % X_SIZE
    sibling = expert + 1 - 2 * (expert % 2)
    across = (expert + 2) % experts
    rows, width = tokens.shape
    hid = param_down.shape[0]
    gu_rows = send_gu.shape[1]
    gu_part = gu_rows // GU_PARTS
    dy_cols = width // DY_PARTS
    blocks = dy_cols // LANES
    down_part = 2 * blocks

    def z_at(j):
        return (z + (j % 2) * ((j + 1) // 2) + (1 - j % 2) * (zs - j // 2)) % zs

    def peer_at(t):
        k = t // zs
        return z_at(t % zs) * plane + ((y + k // X_SIZE) % Y_LO) * X_SIZE + (x + k % X_SIZE) % X_SIZE

    x_cols = width // X_PARTS
    pieces = (
        [(tokens, x_all, pl.ds(c * x_cols, x_cols)) for c in range(X_PARTS)]
        + [(code, codes, None)]
        + [(cotangent, dy_all, pl.ds(c * dy_cols, dy_cols)) for c in range(DY_PARTS)]
    )

    def source(p):
        src, _, cols = pieces[p]
        return src if cols is None else src.at[:, cols]

    def slot(p, s):
        _, dst, cols = pieces[p]
        if cols is None:
            return dst.at[s]
        return dst.at[pl.ds(s * rows, rows), cols]

    loads = [
        pltpu.make_async_copy(param_gu, gu_wide, local_sem.at[0]),
    ]
    for p in range(len(pieces)):
        loads.append(pltpu.make_async_copy(source(p), slot(p, 0), local_sem.at[1 + p]))
    for load in loads:
        load.start()

    def down_load(b):
        cols = pl.ds(pl.multiple_of(b * LANES, LANES), LANES)
        dst = down_wide.at[pl.ds(pl.multiple_of(b * hid, hid), hid)]
        return pltpu.make_async_copy(param_down.at[:, cols], dst, block_sem.at[b])

    @pl.loop(0, width // LANES)
    def _(b):
        down_load(b).start()

    barrier = pltpu.get_barrier_semaphore()
    for other in (sibling, across):
        pl.semaphore_signal(barrier, inc=1, device_id={"expert": other}, device_id_type=MESH)

    @pl.loop(1, nodes)
    def _(t):
        pl.semaphore_signal(barrier, inc=1, device_id={"node": peer_at(t)}, device_id_type=MESH)

    pl.semaphore_wait(barrier, nodes + 1)

    def token_copy(p, way, src, dst, other):
        return pltpu.make_async_remote_copy(
            src_ref=src,
            dst_ref=dst,
            send_sem=tok_send.at[way, p],
            recv_sem=tok_recv.at[way, p],
            device_id={"expert": other},
            device_id_type=MESH,
        )

    to_sibling = [token_copy(p, 0, source(p), slot(p, 1), sibling) for p in range(len(pieces))]
    to_across = [token_copy(p, 1, source(p), slot(p, 2), across) for p in range(len(pieces))]
    onward = [token_copy(p, 2, slot(p, 2), slot(p, 3), sibling) for p in range(len(pieces))]
    for p in range(len(pieces)):
        to_across[p].start()
        to_sibling[p].start()

    loads[0].wait()

    @pl.loop(0, width // TILE)
    def _(k):
        span = pl.ds(pl.multiple_of(k * TILE, TILE), TILE)
        gu_short[span, :] = gu_wide[span, :].astype(jnp.bfloat16)

    @pl.loop(0, width // LANES)
    def _(b):
        down_load(b).wait()
        cols = pl.ds(pl.multiple_of(b * LANES, LANES), LANES)
        block = down_wide[pl.ds(pl.multiple_of(b * hid, hid), hid), :]
        down_short[:, cols] = block.astype(jnp.bfloat16)

    both[...] = jnp.zeros_like(both)
    dact[...] = jnp.zeros_like(dact)

    def arrive(p):
        to_across[p].wait_recv()
        onward[p].start()
        loads[1 + p].wait()
        to_sibling[p].wait_recv()
        onward[p].wait_recv()

    for p in range(X_PARTS):
        arrive(p)

        @pl.loop(p * (x_cols // TILE), (p + 1) * (x_cols // TILE))
        def _(k):
            span = pl.ds(pl.multiple_of(k * TILE, TILE), TILE)
            both[...] += jnp.dot(
                x_all[:, span], gu_short[span, :], preferred_element_type=jnp.float32
            )

    arrive(X_PARTS)
    bit = jnp.where(
        expert == 0, 1, jnp.where(expert == 1, 2, jnp.where(expert == 2, 4, 8))
    ).astype(jnp.int32)

    def picked_at(s):
        wide = jnp.broadcast_to(codes[s][0:1, :], (rows, rows)).T
        return (wide & bit) != 0

    in_scale = 1.0 / math.sqrt(width)
    hid_scale = 1.0 / math.sqrt(hid)
    first = lax.broadcasted_iota(jnp.int32, (hid, hid), 0)
    second = lax.broadcasted_iota(jnp.int32, (hid, hid), 1)
    wanted = jnp.where(first < hid // 2, 2 * first, 2 * first - (hid - 1))
    order = jnp.where(second == wanted, 1.0, 0.0).astype(jnp.bfloat16)
    for s in range(experts):
        part = pl.ds(s * rows, rows)
        gate = both[part, :hid] * in_scale
        upper = both[part, hid:] * in_scale
        act = jnp.where(picked_at(s), gate * jax.nn.sigmoid(gate) * upper, 0.0)
        act_turned[:, part] = lax.dot_general(
            order,
            act.astype(jnp.bfloat16),
            (((1,), (1,)), ((), ())),
            preferred_element_type=jnp.float32,
        ).astype(jnp.bfloat16)

    @pl.loop(0, width // 256)
    def _(k):
        span = pl.ds(pl.multiple_of(k * 256, 256), 256)
        x_turned[span, :] = x_all[:, span].T

    def exchange(t, src, dst, sems, c):
        return pltpu.make_async_remote_copy(
            src_ref=src,
            dst_ref=dst,
            send_sem=sems.at[0, c],
            recv_sem=sems.at[1, c],
            device_id={"node": t},
            device_id_type=MESH,
        )

    def gu_out(peer, c):
        return exchange(
            peer, send_gu.at[peer, pl.ds(c * gu_part, gu_part)], got_gu[c].at[me], gu_sem, c
        )

    def down_out(peer, c):
        return exchange(peer, send_down.at[c, peer], got_down[c].at[me], down_sem, c)

    for c in range(DY_PARTS):
        arrive(X_PARTS + 1 + c)

        @pl.loop(0, dy_cols // TILE)
        def _(k):
            at = pl.multiple_of(c * dy_cols + k * TILE, TILE)
            span = pl.ds(at, TILE)
            dact[...] += lax.dot_general(
                dy_all[:, span],
                down_short[:, span],
                (((1,), (1,)), ((), ())),
                preferred_element_type=jnp.float32,
            )
            grad = jnp.dot(act_turned[...], dy_all[:, span], preferred_element_type=jnp.float32)
            grad = grad * (0.5 * hid_scale)
            for r in range(2):
                for i in range(TILE // LANES):
                    block = c * blocks + k * (TILE // LANES) + i
                    old = down_wide[pl.ds(block * hid + r, nodes, stride=2), :]
                    new = old - grad[r * nodes : (r + 1) * nodes, i * LANES : (i + 1) * LANES]
                    row = r * blocks + k * (TILE // LANES) + i
                    stage[pl.ds(row, nodes, stride=down_part), :] = new

        @pl.loop(0, nodes)
        def _(n):
            span = pl.ds(pl.multiple_of(n * down_part, down_part), down_part)
            send_down[c, n] = stage[span, :].astype(jnp.bfloat16)

        @pl.loop(1, nodes)
        def _(t):
            down_out(peer_at(t), c).start()

        got_down[c][me] = send_down[c, me]

    for s in range(experts):
        part = pl.ds(s * rows, rows)
        gate = both[part, :hid] * in_scale
        upper = both[part, hid:] * in_scale
        sigma = jax.nn.sigmoid(gate)
        da = dact[part, :] * hid_scale
        picked = picked_at(s)
        dgate = da * upper * sigma * (1.0 + gate * (1.0 - sigma))
        dupper = da * gate * sigma
        dboth[part, :hid] = jnp.where(picked, dgate, 0.0).astype(jnp.bfloat16)
        dboth[part, hid:] = jnp.where(picked, dupper, 0.0).astype(jnp.bfloat16)

    @pl.loop(0, zs)
    def _(j):
        zt = z_at(j)
        at = pl.multiple_of(zt * (plane * gu_rows), plane * gu_rows)
        span = pl.ds(at, plane * gu_rows)
        grad = jnp.dot(x_turned[span, :], dboth[...], preferred_element_type=jnp.float32)
        new = gu_wide[span, :] - grad * (0.5 * in_scale)
        send_gu[pl.ds(zt * plane, plane)] = new.astype(jnp.bfloat16).reshape(
            plane, gu_rows, new.shape[1]
        )

        @pl.loop(0, plane)
        def _(k):
            peer = zt * plane + (me + k) % plane

            @pl.when(peer != me)
            def _():
                gu_out(peer, 0).start()

    for c in range(1, GU_PARTS):

        @pl.loop(1, nodes)
        def _(t):
            gu_out(peer_at(t), c).start()

    for c in range(GU_PARTS):
        got_gu[c][me] = send_gu[me, pl.ds(c * gu_part, gu_part)]

    s0, s1, s2, s3 = shifts[0], shifts[1], shifts[2], shifts[3]

    def filtered(got, half, done, mean):
        def wide(index):
            return got[lax.rem(index, nodes)].astype(jnp.float32)

        def early(n, total):
            own = wide(n)
            half[n] = (own + wide(n + s0)) + (wide(n + s1) + wide(n + s0 + s1))
            return total + own

        total = lax.fori_loop(0, nodes, early, jnp.zeros(half.shape[1:], jnp.float32), unroll=2)
        mean[...] = total * (1.0 / nodes)

        def late(n, carry):
            value = (half[n] + half[lax.rem(n + s2, nodes)]) + (
                half[lax.rem(n + s3, nodes)] + half[lax.rem(n + s2 + s3, nodes)]
            )
            done[n] = (value * (1.0 / 16.0)).astype(jnp.bfloat16)
            return carry

        lax.fori_loop(0, nodes, late, 0, unroll=2)

    def gu_home(peer, c):
        dst = out_gu.at[me, pl.ds(c * gu_part, gu_part)]
        return exchange(peer, done_gu.at[c, peer], dst, gu_sem, GU_PARTS + c)

    def down_home(peer, c):
        dst = out_down.at[me, pl.ds(c * down_part, down_part)]
        return exchange(peer, done_down.at[c, peer], dst, down_sem, DY_PARTS + c)

    def whole(got, sems, c):
        most = got.at[pl.ds(0, nodes - 1)]
        return exchange((me + 1) % nodes, most, most, sems, c)

    def own_down(c):
        dst = out_down.at[me, pl.ds(c * down_part, down_part)]
        return pltpu.make_async_copy(done_down.at[c, me], dst, keep_down.at[c])

    def own_gu(c):
        dst = out_gu.at[me, pl.ds(c * gu_part, gu_part)]
        return pltpu.make_async_copy(done_gu.at[c, me], dst, keep_gu.at[c])

    for c in range(DY_PARTS):
        whole(got_down[c], down_sem, c).wait_recv()
        filtered(
            got_down[c],
            half_down,
            done_down.at[c],
            mean_down.at[pl.ds(c * down_part, down_part)],
        )

        @pl.loop(1, nodes)
        def _(t):
            down_home(peer_at(t), c).start()

        own_down(c).start()

    for c in range(GU_PARTS):
        whole(got_gu[c], gu_sem, c).wait_recv()
        filtered(
            got_gu[c], half_gu, done_gu.at[c], mean_gu.at[pl.ds(c * gu_part, gu_part)]
        )

        @pl.loop(1, nodes)
        def _(t):
            gu_home(peer_at(t), c).start()

        own_gu(c).start()

    for p in range(len(pieces)):
        to_sibling[p].wait_send()
        to_across[p].wait_send()
        onward[p].wait_send()
    for c in range(DY_PARTS):
        whole(got_down[c], down_sem, c).wait_send()
        whole(got_down[c], down_sem, DY_PARTS + c).wait_send()
        whole(got_down[c], down_sem, DY_PARTS + c).wait_recv()
        own_down(c).wait()
    for c in range(GU_PARTS):
        whole(got_gu[c], gu_sem, c).wait_send()
        whole(got_gu[c], gu_sem, GU_PARTS + c).wait_send()
        whole(got_gu[c], gu_sem, GU_PARTS + c).wait_recv()
        own_gu(c).wait()


def step(param_gu, param_down, tokens, cotangent, routes, plan):
    nodes = lax.axis_size("node")
    experts = lax.axis_size("expert")
    rows, width = tokens.shape
    cols = param_gu.shape[1]
    hid = param_down.shape[0]
    gu_rows = width // nodes
    down_rows = hid // nodes * width // LANES
    dy_cols = width // DY_PARTS
    down_part = 2 * dy_cols // LANES
    pieces = X_PARTS + 1 + DY_PARTS
    named = jnp.sum(jnp.left_shift(jnp.int32(1), routes), axis=1, dtype=jnp.int32)
    code = jnp.broadcast_to(named[None, :], (8, rows))
    shifts = jnp.left_shift(jnp.int32(1), plan)
    everywhere = pl.BlockSpec(memory_space=pl.ANY)
    inside = pl.BlockSpec(memory_space=pltpu.VMEM)
    short, wide = jnp.bfloat16, jnp.float32

    def body(*refs):
        kernel_body(nodes, *refs)

    mixed_gu, mixed_down, mean_gu, mean_down = pl.pallas_call(
        body,
        out_shape=(
            jax.ShapeDtypeStruct((nodes, gu_rows, cols), short),
            jax.ShapeDtypeStruct((nodes, down_rows, LANES), short),
            jax.ShapeDtypeStruct((gu_rows, cols), wide),
            jax.ShapeDtypeStruct((down_rows, LANES), wide),
        ),
        in_specs=[pl.BlockSpec(memory_space=pltpu.SMEM)] + [everywhere] * 5,
        out_specs=(everywhere, everywhere, inside, inside),
        scratch_shapes=[
            pltpu.VMEM((experts * rows, width), short),
            pltpu.VMEM((experts * rows, width), short),
            pltpu.VMEM((width, experts * rows), short),
            pltpu.VMEM((width, cols), wide),
            pltpu.VMEM((hid * width // LANES, LANES), wide),
            pltpu.VMEM((width, cols), short),
            pltpu.VMEM((hid, width), short),
            pltpu.VMEM((experts * rows, cols), wide),
            pltpu.VMEM((experts * rows, hid), wide),
            pltpu.VMEM((hid, experts * rows), short),
            pltpu.VMEM((experts * rows, cols), short),
            pltpu.VMEM((experts, 8, rows), jnp.int32),
            pltpu.VMEM((nodes * down_part, LANES), wide),
            pltpu.VMEM((nodes, gu_rows // GU_PARTS, cols), wide),
            pltpu.VMEM((nodes, down_part, LANES), wide),
            pltpu.VMEM((nodes, gu_rows, cols), short),
            pltpu.VMEM((DY_PARTS, nodes, down_part, LANES), short),
            pltpu.VMEM((GU_PARTS, nodes, gu_rows // GU_PARTS, cols), short),
            pltpu.VMEM((DY_PARTS, nodes, down_part, LANES), short),
            pltpu.SemaphoreType.DMA((1 + pieces,)),
            pltpu.SemaphoreType.DMA((width // LANES,)),
            pltpu.SemaphoreType.DMA((3, pieces)),
            pltpu.SemaphoreType.DMA((3, pieces)),
            pltpu.SemaphoreType.DMA((2, 2 * GU_PARTS)),
            pltpu.SemaphoreType.DMA((2, 2 * DY_PARTS)),
            pltpu.SemaphoreType.DMA((GU_PARTS,)),
            pltpu.SemaphoreType.DMA((DY_PARTS,)),
        ]
        + [pltpu.VMEM((nodes, gu_rows // GU_PARTS, cols), short)] * GU_PARTS
        + [pltpu.VMEM((nodes, down_part, LANES), short)] * DY_PARTS,
        compiler_params=pltpu.CompilerParams(
            collective_id=1, has_side_effects=True, vmem_limit_bytes=56 * 1024 * 1024
        ),
        name="expert_gossip",
    )(shifts, code, tokens, cotangent, param_gu, param_down)

    def unpacked(value):
        parts = value.reshape(-1, DY_PARTS, 2, dy_cols)
        return jnp.swapaxes(parts, 1, 2).reshape(-1, width)

    return (
        mixed_gu.reshape(width, cols),
        unpacked(mixed_down),
        mean_gu,
        unpacked(mean_down[None]),
    )


def solution(mesh):
    both = P(("node", "expert"), None)
    split = P("node", "expert")
    return jax.shard_map(
        step,
        mesh=mesh,
        in_specs=(split, split, both, both, both, P()),
        out_specs=(split, split, split, split),
        check_vma=False,
    )
```

time: 274 us -> 205 us (0.75)
  waiting for transfers between devices: 70 us -> 0 us
  Pallas kernels: 147 us -> 195 us
  matrix products: 17.6 us -> 0 us
  between operations: 14.2 us -> 0.67 us
  blocking collectives: 9.59 us -> 0 us
  local copies, waits for them, and re-layouts: 14.7 us -> 7.15 us
    all_gather x2 -> x0, waiting for transfers between devices: 68.6 us -> none  [the longest x1 37.6 us: step(): dy = lax.all_gather(cotangent, 'expert', axis=0, tiled=True)]
    pallas_call x1, Pallas kernels: 147 us -> 195 us  [step(): pl.pallas_call(body, out_shape=(jax.ShapeDtypeStruct((nodes, gu_rows, col...]
    dot_general x4 -> x0, matrix products: 17.6 us -> none  [the longest x1 4.8 us: expert_step(): lax.dot_general(x, dboth, (((0,), (0,)), ((), ())), preferred_element_typ...]
    all_gather x1 -> x0, blocking collectives: 9.59 us -> none  [step(): named = lax.all_gather(routes, 'expert', axis=0, tiled=True)]
    convert_element_type x1 -> x0, local copies, waits for them, and re-layouts: 3.27 us -> none  [step(): new_gu.astype(jnp.bfloat16).reshape(nodes, own_gu, lanes)]
    unnamed x11 -> x7, local copies, waits for them, and re-layouts: 5.72 us -> 3.3 us
  transfers between devices with their start and end apart: 2 -> 0, of which waited for: 2 -> 0; matrix products, arithmetic and copies ran while one was open for 4% -> 0% of each run, Pallas kernels for 0% -> 0%
where the time goes in v1:
time: 205 us
  Pallas kernels  195 us (95%)
  local copies, waits for them, and re-layouts  7.15 us (3%)
    pallas_call x1, Pallas kernels, step(): pl.pallas_call(body, out_shape=(jax.ShapeDtypeStruct((nodes, gu_rows, col...  195 us

profile of v1, /device:TPU:1, one launch (start us, length us, event | category | flops | bytes accessed | tf_op | source)
XLA Modules:
  0.0 204.9 jit_solution(8035022915169434976)
XLA Ops:
  0.6 0.7 shift-left_reduce_fusion
  1.3 1.2 broadcast_shift-left_fusion.refs_0_
  2.5 0.6 broadcast_in_dim.2.refs_1_
  3.1 195.2 %expert_gossip.1 = (bf16[64,64,256]{2,1,0:T(8,128)(2,1)}, bf16[64,64,128]{2,1,0:T(8,128)(2,1)}, f32[64,256]{1,0:T(8,128)}, f32[64,128]{1,0:T(8,128)}) custom-call(s32[4]{0:T(128)} %broadcast_shift-left_fusion.refs_0_, s32[8,128]{1,0:T(8,128)} %broadcast_in_dim.2.refs_1_, bf16[128,4096]{1,0:T(8,128)(2,1)} %refs_2_.1, bf16[128,4096]{1,0:T(8,128)(2,1)} %refs_3_.1, ...), custom_call_target="tpu_custom_call" | custom-call | tf_op jit(solution)/shard_map/expert_gossip/pallas_call | solution.py:410
  198.3 1.4 reshape_broadcast_in_dim.3
  199.7 1.3 reshape.22
  201.0 0.0 copy-start
  201.0 0.5 copy.10
  201.6 1.3 copy.12
  202.9 0.0 copy-done
  202.9 0.0 copy-start.1
  202.9 1.3 copy.15
  204.2 0.0 copy-done.1
  204.2 0.6 copy.16
Async XLA Ops:
  201.0 1.9 copy-start
  202.9 1.3 copy-start.1

commit v2 on v1

--- a/solution.py
+++ b/solution.py
@@ -8,6 +8,8 @@
 from jax.sharding import PartitionSpec as P
 
 MESH = pl.DeviceIdType.MESH
+ROUNDS = 4
+SHIFTS = 6
 X_PARTS = 2
 DY_PARTS = 4
 GU_PARTS = 4
@@ -18,8 +20,8 @@
 
 def kernel_body(
     nodes,
-    shifts,
-    code,
+    plan,
+    routes,
     tokens,
     cotangent,
     param_gu,
@@ -41,12 +43,17 @@
     dboth,
     codes,
     stage,
+    turned,
+    mean_stage,
     half_gu,
     half_down,
     send_gu,
     send_down,
     done_gu,
     done_down,
+    home_down,
+    last_down,
+    enter_sem,
     local_sem,
     block_sem,
     tok_send,
@@ -74,17 +81,27 @@
     blocks = dy_cols // LANES
     down_part = 2 * blocks
 
-    def z_at(j):
-        return (z + (j % 2) * ((j + 1) // 2) + (1 - j % 2) * (zs - j // 2)) % zs
-
-    def peer_at(t):
-        k = t // zs
-        return z_at(t % zs) * plane + ((y + k // X_SIZE) % Y_LO) * X_SIZE + (x + k % X_SIZE) % X_SIZE
+    steps = [0] + [d for j in range(1, zs // 2) for d in (j, zs - j)] + [zs // 2]
+    z_bases = [((z + d) % zs) * plane for d in steps]
+
+    def in_plane(k):
+        return ((y + k // X_SIZE) % Y_LO) * X_SIZE + (x + k % X_SIZE) % X_SIZE
+
+    def each_peer(send):
+        @pl.loop(1, plane)
+        def _(k):
+            send(z_bases[0] + in_plane(k))
+
+        @pl.loop(0, plane)
+        def _(k):
+            here = in_plane(k)
+            for base in z_bases[1:]:
+                send(base + here)
 
     x_cols = width // X_PARTS
     pieces = (
         [(tokens, x_all, pl.ds(c * x_cols, x_cols)) for c in range(X_PARTS)]
-        + [(code, codes, None)]
+        + [(routes, codes, None)]
         + [(cotangent, dy_all, pl.ds(c * dy_cols, dy_cols)) for c in range(DY_PARTS)]
     )
 
@@ -103,6 +120,16 @@
     ]
     for p in range(len(pieces)):
         loads.append(pltpu.make_async_copy(source(p), slot(p, 0), local_sem.at[1 + p]))
+    home = me % plane
+    along_z = [((z + d) % zs) * plane + home for d in (1, zs - 1)]
+    along_x = [me - x + (x + d) % X_SIZE for d in (1, X_SIZE - 1)]
+    along_y = [me - y * X_SIZE + (1 - y) * X_SIZE]
+    barrier = pltpu.get_barrier_semaphore()
+    for other in (across, sibling):
+        pl.semaphore_signal(barrier, inc=1, device_id={"expert": other}, device_id_type=MESH)
+    for other in along_z + along_x + along_y:
+        pl.semaphore_signal(barrier, inc=1, device_id={"node": other}, device_id_type=MESH)
+
     for load in loads:
         load.start()
 
@@ -115,15 +142,7 @@
     def _(b):
         down_load(b).start()
 
-    barrier = pltpu.get_barrier_semaphore()
-    for other in (sibling, across):
-        pl.semaphore_signal(barrier, inc=1, device_id={"expert": other}, device_id_type=MESH)
-
-    @pl.loop(1, nodes)
-    def _(t):
-        pl.semaphore_signal(barrier, inc=1, device_id={"node": peer_at(t)}, device_id_type=MESH)
-
-    pl.semaphore_wait(barrier, nodes + 1)
+    pl.semaphore_wait(barrier, 2 + len(along_z + along_x + along_y))
 
     def token_copy(p, way, src, dst, other):
         return pltpu.make_async_remote_copy(
@@ -142,6 +161,14 @@
         to_across[p].start()
         to_sibling[p].start()
 
+    rounds = [along_z] * (zs // 2) + [along_x] * (X_SIZE // 2) + [along_y]
+    for r, others in enumerate(rounds):
+        for other in others:
+            pl.semaphore_signal(
+                enter_sem.at[r], inc=1, device_id={"node": other}, device_id_type=MESH
+            )
+        pl.semaphore_wait(enter_sem.at[r], len(others))
+
     loads[0].wait()
 
     @pl.loop(0, width // TILE)
@@ -177,13 +204,11 @@
             )
 
     arrive(X_PARTS)
-    bit = jnp.where(
-        expert == 0, 1, jnp.where(expert == 1, 2, jnp.where(expert == 2, 4, 8))
-    ).astype(jnp.int32)
 
     def picked_at(s):
-        wide = jnp.broadcast_to(codes[s][0:1, :], (rows, rows)).T
-        return (wide & bit) != 0
+        named = codes[s]
+        hit = jnp.where((named[0:1, :] == expert) | (named[1:2, :] == expert), 1, 0)
+        return jnp.broadcast_to(hit, (rows, rows)).T != 0
 
     in_scale = 1.0 / math.sqrt(width)
     hid_scale = 1.0 / math.sqrt(hid)
@@ -254,9 +279,7 @@
             span = pl.ds(pl.multiple_of(n * down_part, down_part), down_part)
             send_down[c, n] = stage[span, :].astype(jnp.bfloat16)
 
-        @pl.loop(1, nodes)
-        def _(t):
-            down_out(peer_at(t), c).start()
+        each_peer(lambda peer: down_out(peer, c).start())
 
         got_down[c][me] = send_down[c, me]
 
@@ -274,7 +297,7 @@
 
     @pl.loop(0, zs)
     def _(j):
-        zt = z_at(j)
+        zt = (z + (j % 2) * ((j + 1) // 2) + (1 - j % 2) * (zs - j // 2)) % zs
         at = pl.multiple_of(zt * (plane * gu_rows), plane * gu_rows)
         span = pl.ds(at, plane * gu_rows)
         grad = jnp.dot(x_turned[span, :], dboth[...], preferred_element_type=jnp.float32)
@@ -282,25 +305,31 @@
         send_gu[pl.ds(zt * plane, plane)] = new.astype(jnp.bfloat16).reshape(
             plane, gu_rows, new.shape[1]
         )
-
-        @pl.loop(0, plane)
-        def _(k):
-            peer = zt * plane + (me + k) % plane
-
-            @pl.when(peer != me)
-            def _():
+        for k in range(plane):
+            peer = zt * plane + in_plane(k)
+            if k == 0:
+
+                @pl.when(j > 0)
+                def _():
+                    gu_out(peer, 0).start()
+
+            else:
                 gu_out(peer, 0).start()
 
     for c in range(1, GU_PARTS):
 
-        @pl.loop(1, nodes)
-        def _(t):
-            gu_out(peer_at(t), c).start()
+        each_peer(lambda peer: gu_out(peer, c).start())
 
     for c in range(GU_PARTS):
         got_gu[c][me] = send_gu[me, pl.ds(c * gu_part, gu_part)]
 
-    s0, s1, s2, s3 = shifts[0], shifts[1], shifts[2], shifts[3]
+    def shift_at(i):
+        exponent, shift = plan[i], jnp.int32(1)
+        for e in range(1, SHIFTS):
+            shift = jnp.where(exponent == e, jnp.int32(1 << e), shift)
+        return shift
+
+    s0, s1, s2, s3 = (shift_at(i) for i in range(ROUNDS))
 
     def filtered(got, half, done, mean):
         def wide(index):
@@ -328,16 +357,17 @@
         return exchange(peer, done_gu.at[c, peer], dst, gu_sem, GU_PARTS + c)
 
     def down_home(peer, c):
-        dst = out_down.at[me, pl.ds(c * down_part, down_part)]
-        return exchange(peer, done_down.at[c, peer], dst, down_sem, DY_PARTS + c)
+        return exchange(
+            peer, done_down.at[c, peer], home_down.at[c, me], down_sem, DY_PARTS + c
+        )
 
     def whole(got, sems, c):
         most = got.at[pl.ds(0, nodes - 1)]
         return exchange((me + 1) % nodes, most, most, sems, c)
 
-    def own_down(c):
-        dst = out_down.at[me, pl.ds(c * down_part, down_part)]
-        return pltpu.make_async_copy(done_down.at[c, me], dst, keep_down.at[c])
+    def put_down(c):
+        cols = pl.ds(c * dy_cols, dy_cols)
+        return pltpu.make_async_copy(last_down.at[c], out_down.at[:, cols], keep_down.at[c])
 
     def own_gu(c):
         dst = out_gu.at[me, pl.ds(c * gu_part, gu_part)]
@@ -349,14 +379,18 @@
             got_down[c],
             half_down,
             done_down.at[c],
-            mean_down.at[pl.ds(c * down_part, down_part)],
-        )
-
-        @pl.loop(1, nodes)
-        def _(t):
-            down_home(peer_at(t), c).start()
-
-        own_down(c).start()
+            mean_stage,
+        )
+        for r in range(2):
+            for i in range(blocks):
+                at = c * dy_cols + i * LANES
+                mean_down[r : r + 1, at : at + LANES] = mean_stage[
+                    r * blocks + i : r * blocks + i + 1, :
+                ]
+
+        each_peer(lambda peer: down_home(peer, c).start())
+
+        home_down[c, me] = done_down[c, me]
 
     for c in range(GU_PARTS):
         whole(got_gu[c], gu_sem, c).wait_recv()
@@ -364,11 +398,28 @@
             got_gu[c], half_gu, done_gu.at[c], mean_gu.at[pl.ds(c * gu_part, gu_part)]
         )
 
-        @pl.loop(1, nodes)
-        def _(t):
-            gu_home(peer_at(t), c).start()
+        each_peer(lambda peer: gu_home(peer, c).start())
 
         own_gu(c).start()
+
+    for c in range(DY_PARTS):
+        whole(got_down[c], down_sem, DY_PARTS + c).wait_recv()
+
+        @pl.loop(0, nodes)
+        def _(n):
+            span = pl.ds(pl.multiple_of(n * down_part, down_part), down_part)
+            stage[span, :] = home_down[c, n].astype(jnp.float32)
+
+        for i in range(blocks):
+            for r in range(2):
+                row = r * blocks + i
+                turned[pl.ds(i * hid + r, nodes, stride=2), :] = stage[
+                    pl.ds(row, nodes, stride=down_part), :
+                ]
+            last_down[c, :, i * LANES : (i + 1) * LANES] = turned[
+                i * hid : (i + 1) * hid, :
+            ].astype(jnp.bfloat16)
+        put_down(c).start()
 
     for p in range(len(pieces)):
         to_sibling[p].wait_send()
@@ -377,8 +428,7 @@
     for c in range(DY_PARTS):
         whole(got_down[c], down_sem, c).wait_send()
         whole(got_down[c], down_sem, DY_PARTS + c).wait_send()
-        whole(got_down[c], down_sem, DY_PARTS + c).wait_recv()
-        own_down(c).wait()
+        put_down(c).wait()
     for c in range(GU_PARTS):
         whole(got_gu[c], gu_sem, c).wait_send()
         whole(got_gu[c], gu_sem, GU_PARTS + c).wait_send()
@@ -393,13 +443,9 @@
     cols = param_gu.shape[1]
     hid = param_down.shape[0]
     gu_rows = width // nodes
-    down_rows = hid // nodes * width // LANES
     dy_cols = width // DY_PARTS
     down_part = 2 * dy_cols // LANES
     pieces = X_PARTS + 1 + DY_PARTS
-    named = jnp.sum(jnp.left_shift(jnp.int32(1), routes), axis=1, dtype=jnp.int32)
-    code = jnp.broadcast_to(named[None, :], (8, rows))
-    shifts = jnp.left_shift(jnp.int32(1), plan)
     everywhere = pl.BlockSpec(memory_space=pl.ANY)
     inside = pl.BlockSpec(memory_space=pltpu.VMEM)
     short, wide = jnp.bfloat16, jnp.float32
@@ -411,9 +457,9 @@
         body,
         out_shape=(
             jax.ShapeDtypeStruct((nodes, gu_rows, cols), short),
-            jax.ShapeDtypeStruct((nodes, down_rows, LANES), short),
+            jax.ShapeDtypeStruct((hid, width), short),
             jax.ShapeDtypeStruct((gu_rows, cols), wide),
-            jax.ShapeDtypeStruct((down_rows, LANES), wide),
+            jax.ShapeDtypeStruct((hid // nodes, width), wide),
         ),
         in_specs=[pl.BlockSpec(memory_space=pltpu.SMEM)] + [everywhere] * 5,
         out_specs=(everywhere, everywhere, inside, inside),
@@ -429,14 +475,19 @@
             pltpu.VMEM((experts * rows, hid), wide),
             pltpu.VMEM((hid, experts * rows), short),
             pltpu.VMEM((experts * rows, cols), short),
-            pltpu.VMEM((experts, 8, rows), jnp.int32),
+            pltpu.VMEM((experts, 2, rows), jnp.int32),
             pltpu.VMEM((nodes * down_part, LANES), wide),
+            pltpu.VMEM((nodes * down_part, LANES), wide),
+            pltpu.VMEM((down_part, LANES), wide),
             pltpu.VMEM((nodes, gu_rows // GU_PARTS, cols), wide),
             pltpu.VMEM((nodes, down_part, LANES), wide),
             pltpu.VMEM((nodes, gu_rows, cols), short),
             pltpu.VMEM((DY_PARTS, nodes, down_part, LANES), short),
             pltpu.VMEM((GU_PARTS, nodes, gu_rows // GU_PARTS, cols), short),
             pltpu.VMEM((DY_PARTS, nodes, down_part, LANES), short),
+            pltpu.VMEM((DY_PARTS, nodes, down_part, LANES), short),
+            pltpu.VMEM((DY_PARTS, hid, dy_cols), short),
+            pltpu.SemaphoreType.REGULAR((nodes // (Y_LO * X_SIZE) // 2 + X_SIZE // 2 + 1,)),
             pltpu.SemaphoreType.DMA((1 + pieces,)),
             pltpu.SemaphoreType.DMA((width // LANES,)),
             pltpu.SemaphoreType.DMA((3, pieces)),
@@ -452,18 +503,9 @@
             collective_id=1, has_side_effects=True, vmem_limit_bytes=56 * 1024 * 1024
         ),
         name="expert_gossip",
-    )(shifts, code, tokens, cotangent, param_gu, param_down)
-
-    def unpacked(value):
-        parts = value.reshape(-1, DY_PARTS, 2, dy_cols)
-        return jnp.swapaxes(parts, 1, 2).reshape(-1, width)
-
-    return (
-        mixed_gu.reshape(width, cols),
-        unpacked(mixed_down),
-        mean_gu,
-        unpacked(mean_down[None]),
-    )
+    )(plan, routes.T, tokens, cotangent, param_gu, param_down)
+
+    return mixed_gu.reshape(width, cols), mixed_down, mean_gu, mean_down
 
 
 def solution(mesh):

time: 205 us -> 196 us (0.956)
  Pallas kernels: 195 us -> 190 us
    pallas_call x1, Pallas kernels: 195 us -> 190 us  [step(): pl.pallas_call(body, out_shape=(jax.ShapeDtypeStruct((nodes, gu_rows, col...]
    unnamed x7 -> x10, local copies, waits for them, and re-layouts: 3.3 us -> 5.36 us
where the time goes in v2:
time: 196 us
  Pallas kernels  190 us (97%)
  local copies, waits for them, and re-layouts  5.36 us (3%)
    pallas_call x1, Pallas kernels, step(): pl.pallas_call(body, out_shape=(jax.ShapeDtypeStruct((nodes, gu_rows, col...  190 us
    unnamed x10, local copies, waits for them, and re-layouts  5.36 us

profile of v2, /device:TPU:1, one launch (start us, length us, event | category | flops | bytes accessed | tf_op | source)
XLA Modules:
  0.0 195.7 jit_solution(3894034973697739060)
XLA Ops:
  0.6 189.7 %expert_gossip.1 = (bf16[64,64,256]{2,1,0:T(8,128)(2,1)}, bf16[128,4096]{1,0:T(8,128)(2,1)}, f32[64,256]{1,0:T(8,128)}, f32[2,4096]{1,0:T(2,128)}) custom-call(s32[4]{0:T(128)} %refs_0_.1, s32[2,128]{1,0:T(2,128)} %bitcast.3, bf16[128,4096]{1,0:T(8,128)(2,1)} %refs_2_.1, bf16[128,4096]{1,0:T(8,128)(2,1)} %refs_3_.1, f32[4096,256]{1,0:T(8,128)} %refs_4_.1, ...), custom_call_target="tpu_custom_call" | custom-call | tf_op jit(solution)/shard_map/expert_gossip/pallas_call | solution.py:456
  190.4 0.0 copy-start
  190.4 3.1 %copy.14 = bf16[4096,256]{1,0:T(8,128)(2,1)} copy(bf16[4096,256]{1,0:T(8,128)(2,1)} %bitcast.2) | data formatting | bytes 4194304
  193.5 0.0 copy-done
  193.5 0.0 copy-start.1
  193.5 0.0 copy-start.2
  193.5 1.0 copy.15
  194.5 0.0 copy-done.1
  194.5 0.6 copy.16
  195.1 0.0 copy-done.2
  195.1 0.6 copy.17
Async XLA Ops:
  190.4 3.1 %copy-start = (bf16[128,4096]{1,0:T(8,128)(2,1)S(1)}, bf16[128,4096]{1,0:T(8,128)(2,1)}, u32[]{:S(2)}) copy-start(bf16[128,4096]{1,0:T(8,128)(2,1)} %get-tuple-element.17) | copy-start | bytes 3145732
  193.5 1.0 copy-start.1
  193.5 1.6 copy-start.2

commit v3 on v2

--- a/solution.py
+++ b/solution.py
@@ -11,7 +11,8 @@
 ROUNDS = 4
 SHIFTS = 6
 X_PARTS = 2
-DY_PARTS = 4
+DY_BLOCKS = (4, 4, 8, 8, 8)
+DY_PARTS = len(DY_BLOCKS)
 GU_PARTS = 4
 LANES = 128
 TILE = 512
@@ -45,14 +46,13 @@
     stage,
     turned,
     mean_stage,
+    mean_rows,
+    mean_slab,
+    mean_sem,
     half_gu,
     half_down,
     send_gu,
-    send_down,
     done_gu,
-    done_down,
-    home_down,
-    last_down,
     enter_sem,
     local_sem,
     block_sem,
@@ -64,7 +64,10 @@
     keep_down,
     *landing,
 ):
-    got_gu, got_down = landing[:GU_PARTS], landing[GU_PARTS:]
+    got_gu, downs = landing[:GU_PARTS], landing[GU_PARTS:]
+    send_down, got_down, done_down, home_down, last_down = (
+        downs[i * DY_PARTS : (i + 1) * DY_PARTS] for i in range(5)
+    )
     me = lax.axis_index("node")
     expert = lax.axis_index("expert")
     experts = lax.axis_size("expert")
@@ -77,9 +80,7 @@
     hid = param_down.shape[0]
     gu_rows = send_gu.shape[1]
     gu_part = gu_rows // GU_PARTS
-    dy_cols = width // DY_PARTS
-    blocks = dy_cols // LANES
-    down_part = 2 * blocks
+    starts = [sum(DY_BLOCKS[:c]) for c in range(DY_PARTS)]
 
     steps = [0] + [d for j in range(1, zs // 2) for d in (j, zs - j)] + [zs // 2]
     z_bases = [((z + d) % zs) * plane for d in steps]
@@ -100,9 +101,12 @@
 
     x_cols = width // X_PARTS
     pieces = (
-        [(tokens, x_all, pl.ds(c * x_cols, x_cols)) for c in range(X_PARTS)]
-        + [(routes, codes, None)]
-        + [(cotangent, dy_all, pl.ds(c * dy_cols, dy_cols)) for c in range(DY_PARTS)]
+        [(routes, codes, None)]
+        + [(tokens, x_all, pl.ds(c * x_cols, x_cols)) for c in range(X_PARTS)]
+        + [
+            (cotangent, dy_all, pl.ds(starts[c] * LANES, DY_BLOCKS[c] * LANES))
+            for c in range(DY_PARTS)
+        ]
     )
 
     def source(p):
@@ -116,10 +120,9 @@
         return dst.at[pl.ds(s * rows, rows), cols]
 
     loads = [
-        pltpu.make_async_copy(param_gu, gu_wide, local_sem.at[0]),
+        pltpu.make_async_copy(source(p), slot(p, 0), local_sem.at[p]) for p in range(len(pieces))
     ]
-    for p in range(len(pieces)):
-        loads.append(pltpu.make_async_copy(source(p), slot(p, 0), local_sem.at[1 + p]))
+    loads.append(pltpu.make_async_copy(param_gu, gu_wide, local_sem.at[len(pieces)]))
     home = me % plane
     along_z = [((z + d) % zs) * plane + home for d in (1, zs - 1)]
     along_x = [me - x + (x + d) % X_SIZE for d in (1, X_SIZE - 1)]
@@ -154,10 +157,11 @@
             device_id_type=MESH,
         )
 
-    to_sibling = [token_copy(p, 0, source(p), slot(p, 1), sibling) for p in range(len(pieces))]
-    to_across = [token_copy(p, 1, source(p), slot(p, 2), across) for p in range(len(pieces))]
+    to_sibling = [token_copy(p, 0, slot(p, 0), slot(p, 1), sibling) for p in range(len(pieces))]
+    to_across = [token_copy(p, 1, slot(p, 0), slot(p, 2), across) for p in range(len(pieces))]
     onward = [token_copy(p, 2, slot(p, 2), slot(p, 3), sibling) for p in range(len(pieces))]
     for p in range(len(pieces)):
+        loads[p].wait()
         to_across[p].start()
         to_sibling[p].start()
 
@@ -169,7 +173,7 @@
             )
         pl.semaphore_wait(enter_sem.at[r], len(others))
 
-    loads[0].wait()
+    loads[-1].wait()
 
     @pl.loop(0, width // TILE)
     def _(k):
@@ -189,12 +193,12 @@
     def arrive(p):
         to_across[p].wait_recv()
         onward[p].start()
-        loads[1 + p].wait()
         to_sibling[p].wait_recv()
         onward[p].wait_recv()
 
+    arrive(0)
     for p in range(X_PARTS):
-        arrive(p)
+        arrive(1 + p)
 
         @pl.loop(p * (x_cols // TILE), (p + 1) * (x_cols // TILE))
         def _(k):
@@ -202,8 +206,6 @@
             both[...] += jnp.dot(
                 x_all[:, span], gu_short[span, :], preferred_element_type=jnp.float32
             )
-
-    arrive(X_PARTS)
 
     def picked_at(s):
         named = codes[s]
@@ -249,14 +251,16 @@
         )
 
     def down_out(peer, c):
-        return exchange(peer, send_down.at[c, peer], got_down[c].at[me], down_sem, c)
+        return exchange(peer, send_down[c].at[peer], got_down[c].at[me], down_sem, c)
 
     for c in range(DY_PARTS):
-        arrive(X_PARTS + 1 + c)
-
-        @pl.loop(0, dy_cols // TILE)
+        arrive(1 + X_PARTS + c)
+        blocks = DY_BLOCKS[c]
+        down_part = 2 * blocks
+
+        @pl.loop(0, blocks * LANES // TILE)
         def _(k):
-            at = pl.multiple_of(c * dy_cols + k * TILE, TILE)
+            at = pl.multiple_of(starts[c] * LANES + k * TILE, TILE)
             span = pl.ds(at, TILE)
             dact[...] += lax.dot_general(
                 dy_all[:, span],
@@ -268,7 +272,7 @@
             grad = grad * (0.5 * hid_scale)
             for r in range(2):
                 for i in range(TILE // LANES):
-                    block = c * blocks + k * (TILE // LANES) + i
+                    block = starts[c] + k * (TILE // LANES) + i
                     old = down_wide[pl.ds(block * hid + r, nodes, stride=2), :]
                     new = old - grad[r * nodes : (r + 1) * nodes, i * LANES : (i + 1) * LANES]
                     row = r * blocks + k * (TILE // LANES) + i
@@ -277,11 +281,11 @@
         @pl.loop(0, nodes)
         def _(n):
             span = pl.ds(pl.multiple_of(n * down_part, down_part), down_part)
-            send_down[c, n] = stage[span, :].astype(jnp.bfloat16)
+            send_down[c][n] = stage[span, :].astype(jnp.bfloat16)
 
         each_peer(lambda peer: down_out(peer, c).start())
 
-        got_down[c][me] = send_down[c, me]
+        got_down[c][me] = send_down[c][me]
 
     for s in range(experts):
         part = pl.ds(s * rows, rows)
@@ -358,7 +362,7 @@
 
     def down_home(peer, c):
         return exchange(
-            peer, done_down.at[c, peer], home_down.at[c, me], down_sem, DY_PARTS + c
+            peer, done_down[c].at[peer], home_down[c].at[me], down_sem, DY_PARTS + c
         )
 
     def whole(got, sems, c):
@@ -366,8 +370,8 @@
         return exchange((me + 1) % nodes, most, most, sems, c)
 
     def put_down(c):
-        cols = pl.ds(c * dy_cols, dy_cols)
-        return pltpu.make_async_copy(last_down.at[c], out_down.at[:, cols], keep_down.at[c])
+        cols = pl.ds(starts[c] * LANES, DY_BLOCKS[c] * LANES)
+        return pltpu.make_async_copy(last_down[c], out_down.at[:, cols], keep_down.at[c])
 
     def own_gu(c):
         dst = out_gu.at[me, pl.ds(c * gu_part, gu_part)]
@@ -375,40 +379,50 @@
 
     for c in range(DY_PARTS):
         whole(got_down[c], down_sem, c).wait_recv()
+        blocks = DY_BLOCKS[c]
         filtered(
             got_down[c],
-            half_down,
-            done_down.at[c],
-            mean_stage,
+            half_down.at[:, pl.ds(0, 2 * blocks)],
+            done_down[c],
+            mean_stage.at[pl.ds(0, 2 * blocks)],
         )
         for r in range(2):
             for i in range(blocks):
-                at = c * dy_cols + i * LANES
-                mean_down[r : r + 1, at : at + LANES] = mean_stage[
+                at = (starts[c] + i) * LANES
+                mean_rows[r : r + 1, at : at + LANES] = mean_stage[
                     r * blocks + i : r * blocks + i + 1, :
                 ]
 
         each_peer(lambda peer: down_home(peer, c).start())
 
-        home_down[c, me] = done_down[c, me]
+        home_down[c][me] = done_down[c][me]
 
     for c in range(GU_PARTS):
         whole(got_gu[c], gu_sem, c).wait_recv()
         filtered(
-            got_gu[c], half_gu, done_gu.at[c], mean_gu.at[pl.ds(c * gu_part, gu_part)]
+            got_gu[c], half_gu, done_gu.at[c], mean_slab.at[pl.ds(c * gu_part, gu_part)]
         )
 
         each_peer(lambda peer: gu_home(peer, c).start())
 
         own_gu(c).start()
+
+    means = [
+        pltpu.make_async_copy(mean_slab, mean_gu, mean_sem.at[0]),
+        pltpu.make_async_copy(mean_rows, mean_down, mean_sem.at[1]),
+    ]
+    for copy in means:
+        copy.start()
 
     for c in range(DY_PARTS):
         whole(got_down[c], down_sem, DY_PARTS + c).wait_recv()
+        blocks = DY_BLOCKS[c]
+        down_part = 2 * blocks
 
         @pl.loop(0, nodes)
         def _(n):
             span = pl.ds(pl.multiple_of(n * down_part, down_part), down_part)
-            stage[span, :] = home_down[c, n].astype(jnp.float32)
+            stage[span, :] = home_down[c][n].astype(jnp.float32)
 
         for i in range(blocks):
             for r in range(2):
@@ -416,11 +430,13 @@
                 turned[pl.ds(i * hid + r, nodes, stride=2), :] = stage[
                     pl.ds(row, nodes, stride=down_part), :
                 ]
-            last_down[c, :, i * LANES : (i + 1) * LANES] = turned[
+            last_down[c][:, i * LANES : (i + 1) * LANES] = turned[
                 i * hid : (i + 1) * hid, :
             ].astype(jnp.bfloat16)
         put_down(c).start()
 
+    for copy in means:
+        copy.wait()
     for p in range(len(pieces)):
         to_sibling[p].wait_send()
         to_across[p].wait_send()
@@ -443,16 +459,19 @@
     cols = param_gu.shape[1]
     hid = param_down.shape[0]
     gu_rows = width // nodes
-    dy_cols = width // DY_PARTS
-    down_part = 2 * dy_cols // LANES
+    down_part = 2 * max(DY_BLOCKS)
     pieces = X_PARTS + 1 + DY_PARTS
     everywhere = pl.BlockSpec(memory_space=pl.ANY)
-    inside = pl.BlockSpec(memory_space=pltpu.VMEM)
+    outside = pl.BlockSpec(memory_space=pltpu.HBM)
     short, wide = jnp.bfloat16, jnp.float32
 
     def body(*refs):
         kernel_body(nodes, *refs)
 
+    held = [
+        pltpu.with_memory_space_constraint(a, pltpu.HBM)
+        for a in (routes.T, tokens, cotangent, param_gu, param_down)
+    ]
     mixed_gu, mixed_down, mean_gu, mean_down = pl.pallas_call(
         body,
         out_shape=(
@@ -461,8 +480,8 @@
             jax.ShapeDtypeStruct((gu_rows, cols), wide),
             jax.ShapeDtypeStruct((hid // nodes, width), wide),
         ),
-        in_specs=[pl.BlockSpec(memory_space=pltpu.SMEM)] + [everywhere] * 5,
-        out_specs=(everywhere, everywhere, inside, inside),
+        in_specs=[pl.BlockSpec(memory_space=pltpu.SMEM)] + [outside] * 5,
+        out_specs=(everywhere,) * 4,
         scratch_shapes=[
             pltpu.VMEM((experts * rows, width), short),
             pltpu.VMEM((experts * rows, width), short),
@@ -479,14 +498,13 @@
             pltpu.VMEM((nodes * down_part, LANES), wide),
             pltpu.VMEM((nodes * down_part, LANES), wide),
             pltpu.VMEM((down_part, LANES), wide),
+            pltpu.VMEM((hid // nodes, width), wide),
+            pltpu.VMEM((gu_rows, cols), wide),
+            pltpu.SemaphoreType.DMA((2,)),
             pltpu.VMEM((nodes, gu_rows // GU_PARTS, cols), wide),
             pltpu.VMEM((nodes, down_part, LANES), wide),
             pltpu.VMEM((nodes, gu_rows, cols), short),
-            pltpu.VMEM((DY_PARTS, nodes, down_part, LANES), short),
             pltpu.VMEM((GU_PARTS, nodes, gu_rows // GU_PARTS, cols), short),
-            pltpu.VMEM((DY_PARTS, nodes, down_part, LANES), short),
-            pltpu.VMEM((DY_PARTS, nodes, down_part, LANES), short),
-            pltpu.VMEM((DY_PARTS, hid, dy_cols), short),
             pltpu.SemaphoreType.REGULAR((nodes // (Y_LO * X_SIZE) // 2 + X_SIZE // 2 + 1,)),
             pltpu.SemaphoreType.DMA((1 + pieces,)),
             pltpu.SemaphoreType.DMA((width // LANES,)),
@@ -498,12 +516,13 @@
             pltpu.SemaphoreType.DMA((DY_PARTS,)),
         ]
         + [pltpu.VMEM((nodes, gu_rows // GU_PARTS, cols), short)] * GU_PARTS
-        + [pltpu.VMEM((nodes, down_part, LANES), short)] * DY_PARTS,
+        + [pltpu.VMEM((nodes, 2 * b, LANES), short) for b in DY_BLOCKS] * 4
+        + [pltpu.VMEM((hid, b * LANES), short) for b in DY_BLOCKS],
         compiler_params=pltpu.CompilerParams(
-            collective_id=1, has_side_effects=True, vmem_limit_bytes=56 * 1024 * 1024
+            collective_id=1, has_side_effects=True, vmem_limit_bytes=48 * 1024 * 1024
         ),
         name="expert_gossip",
-    )(plan, routes.T, tokens, cotangent, param_gu, param_down)
+    )(plan, *held)
 
     return mixed_gu.reshape(width, cols), mixed_down, mean_gu, mean_down
 

time: 196 us -> 194 us (0.990)
    unnamed x10 -> x6, local copies, waits for them, and re-layouts: 5.36 us -> 4.18 us
where the time goes in v3:
time: 194 us
  Pallas kernels  189 us (97%)
  local copies, waits for them, and re-layouts  4.18 us (2%)
    pallas_call x1, Pallas kernels, step(): pl.pallas_call(body, out_shape=(jax.ShapeDtypeStruct((nodes, gu_rows, col...  189 us
    unnamed x6, local copies, waits for them, and re-layouts  4.18 us

profile of v3, /device:TPU:1, one launch (start us, length us, event | category | flops | bytes accessed | tf_op | source)
XLA Modules:
  0.0 193.7 jit_solution(16315850213186540190)
XLA Ops:
  0.6 0.0 copy-start
  0.6 0.6 copy-done
  1.3 188.8 %expert_gossip.1 = (bf16[64,64,256]{2,1,0:T(8,128)(2,1)S(1)}, bf16[128,4096]{1,0:T(8,128)(2,1)S(1)}, f32[64,256]{1,0:T(8,128)S(1)}, f32[2,4096]{1,0:T(2,128)S(1)}) custom-call(s32[4]{0:T(128)S(1)} %copy-done, s32[2,128]{1,0:T(2,128)} %bitcast.3, bf16[128,4096]{1,0:T(8,128)(2,1)} %refs_2_.1, bf16[128,4096]{1,0:T(8,128)(2,1)} %refs_3_.1, f32[4096,256]{1,0:T(8,128)} %refs_4_.1, ...), custom_call_target="tpu_custom_call" | custom-call | tf_op jit(solution)/shard_map/expert_gossip/pallas_call | solution.py:475
  190.1 1.3 copy.14
  191.5 1.0 copy.15
  192.4 0.6 copy.16
  193.1 0.6 copy.17
Async XLA Ops:
  0.6 0.7 copy-start

commit v4 on v3

--- a/solution.py
+++ b/solution.py
@@ -10,7 +10,7 @@
 MESH = pl.DeviceIdType.MESH
 ROUNDS = 4
 SHIFTS = 6
-X_PARTS = 2
+X_PARTS = 4
 DY_BLOCKS = (4, 4, 8, 8, 8)
 DY_PARTS = len(DY_BLOCKS)
 GU_PARTS = 4
@@ -60,13 +60,15 @@
     tok_recv,
     gu_sem,
     down_sem,
+    relay_sem,
+    over_sem,
     keep_gu,
     keep_down,
     *landing,
 ):
     got_gu, downs = landing[:GU_PARTS], landing[GU_PARTS:]
-    send_down, got_down, done_down, home_down, last_down = (
-        downs[i * DY_PARTS : (i + 1) * DY_PARTS] for i in range(5)
+    send_down, got_down, done_down, home_down, relay_down, last_down = (
+        downs[i * DY_PARTS : (i + 1) * DY_PARTS] for i in range(6)
     )
     me = lax.axis_index("node")
     expert = lax.axis_index("expert")
@@ -196,6 +198,12 @@
         to_sibling[p].wait_recv()
         onward[p].wait_recv()
 
+    def turn(p):
+        @pl.loop(p * (x_cols // 256), (p + 1) * (x_cols // 256))
+        def _(k):
+            span = pl.ds(pl.multiple_of(k * 256, 256), 256)
+            x_turned[span, :] = x_all[:, span].T
+
     arrive(0)
     for p in range(X_PARTS):
         arrive(1 + p)
@@ -206,6 +214,9 @@
             both[...] += jnp.dot(
                 x_all[:, span], gu_short[span, :], preferred_element_type=jnp.float32
             )
+
+        if p < X_PARTS - 1:
+            turn(p)
 
     def picked_at(s):
         named = codes[s]
@@ -230,11 +241,6 @@
             preferred_element_type=jnp.float32,
         ).astype(jnp.bfloat16)
 
-    @pl.loop(0, width // 256)
-    def _(k):
-        span = pl.ds(pl.multiple_of(k * 256, 256), 256)
-        x_turned[span, :] = x_all[:, span].T
-
     def exchange(t, src, dst, sems, c):
         return pltpu.make_async_remote_copy(
             src_ref=src,
@@ -250,8 +256,46 @@
             peer, send_gu.at[peer, pl.ds(c * gu_part, gu_part)], got_gu[c].at[me], gu_sem, c
         )
 
+    spot = z * X_SIZE + x
+    over = along_y[0]
+
+    def some(ref, first, count, sems, c):
+        most = ref.at[pl.ds(first, count)]
+        return exchange((me + 1) % nodes, most, most, sems, c)
+
+    def whole(got, sems, c):
+        return some(got, 0, nodes - 1, sems, c)
+
     def down_out(peer, c):
         return exchange(peer, send_down[c].at[peer], got_down[c].at[me], down_sem, c)
+
+    def down_relay(peer, c):
+        other = peer - y * X_SIZE + (1 - y) * X_SIZE
+        return exchange(peer, send_down[c].at[other], relay_down[c].at[spot], relay_sem, c)
+
+    def down_over(k, c):
+        return exchange(
+            over,
+            relay_down[c].at[pl.ds(k * X_SIZE, X_SIZE)],
+            got_down[c].at[pl.ds(k * plane + y * X_SIZE, X_SIZE)],
+            over_sem,
+            c,
+        )
+
+    def send_row(c):
+        def both_ways(peer):
+            down_out(peer, c).start()
+            down_relay(peer, c).start()
+
+        @pl.loop(1, X_SIZE)
+        def _(k):
+            both_ways(z_bases[0] + y * X_SIZE + (x + k) % X_SIZE)
+
+        @pl.loop(0, X_SIZE)
+        def _(k):
+            here = y * X_SIZE + (x + k) % X_SIZE
+            for base in z_bases[1:]:
+                both_ways(base + here)
 
     for c in range(DY_PARTS):
         arrive(1 + X_PARTS + c)
@@ -283,9 +327,11 @@
             span = pl.ds(pl.multiple_of(n * down_part, down_part), down_part)
             send_down[c][n] = stage[span, :].astype(jnp.bfloat16)
 
-        each_peer(lambda peer: down_out(peer, c).start())
-
+        send_row(c)
         got_down[c][me] = send_down[c][me]
+        relay_down[c][spot] = send_down[c][over]
+        if c == 1:
+            turn(X_PARTS - 1)
 
     for s in range(experts):
         part = pl.ds(s * rows, rows)
@@ -320,6 +366,13 @@
             else:
                 gu_out(peer, 0).start()
 
+    for c in range(DY_PARTS):
+        some(relay_down[c], 1, nodes // Y_LO - 1, relay_sem, c).wait_recv()
+
+        @pl.loop(0, zs)
+        def _(k):
+            down_over(k, c).start()
+
     for c in range(1, GU_PARTS):
 
         each_peer(lambda peer: gu_out(peer, c).start())
@@ -365,10 +418,6 @@
             peer, done_down[c].at[peer], home_down[c].at[me], down_sem, DY_PARTS + c
         )
 
-    def whole(got, sems, c):
-        most = got.at[pl.ds(0, nodes - 1)]
-        return exchange((me + 1) % nodes, most, most, sems, c)
-
     def put_down(c):
         cols = pl.ds(starts[c] * LANES, DY_BLOCKS[c] * LANES)
         return pltpu.make_async_copy(last_down[c], out_down.at[:, cols], keep_down.at[c])
@@ -378,7 +427,8 @@
         return pltpu.make_async_copy(done_gu.at[c, me], dst, keep_gu.at[c])
 
     for c in range(DY_PARTS):
-        whole(got_down[c], down_sem, c).wait_recv()
+        some(got_down[c], 0, nodes // Y_LO - 1, down_sem, c).wait_recv()
+        some(got_down[c], 0, nodes // Y_LO, over_sem, c).wait_recv()
         blocks = DY_BLOCKS[c]
         filtered(
             got_down[c],
@@ -442,7 +492,9 @@
         to_across[p].wait_send()
         onward[p].wait_send()
     for c in range(DY_PARTS):
-        whole(got_down[c], down_sem, c).wait_send()
+        some(got_down[c], 0, nodes // Y_LO - 1, down_sem, c).wait_send()
+        some(relay_down[c], 1, nodes // Y_LO - 1, relay_sem, c).wait_send()
+        some(got_down[c], 0, nodes // Y_LO, over_sem, c).wait_send()
         whole(got_down[c], down_sem, DY_PARTS + c).wait_send()
         put_down(c).wait()
     for c in range(GU_PARTS):
@@ -450,6 +502,15 @@
         whole(got_gu[c], gu_sem, GU_PARTS + c).wait_send()
         whole(got_gu[c], gu_sem, GU_PARTS + c).wait_recv()
         own_gu(c).wait()
+
+
+def put_out(*refs):
+    sems = refs[-1]
+    copies = [pltpu.make_async_copy(refs[i], refs[4 + i], sems.at[i]) for i in range(4)]
+    for copy in copies:
+        copy.start()
+    for copy in copies:
+        copy.wait()
 
 
 def step(param_gu, param_down, tokens, cotangent, routes, plan):
@@ -512,11 +573,14 @@
             pltpu.SemaphoreType.DMA((3, pieces)),
             pltpu.SemaphoreType.DMA((2, 2 * GU_PARTS)),
             pltpu.SemaphoreType.DMA((2, 2 * DY_PARTS)),
+            pltpu.SemaphoreType.DMA((2, DY_PARTS)),
+            pltpu.SemaphoreType.DMA((2, DY_PARTS)),
             pltpu.SemaphoreType.DMA((GU_PARTS,)),
             pltpu.SemaphoreType.DMA((DY_PARTS,)),
         ]
         + [pltpu.VMEM((nodes, gu_rows // GU_PARTS, cols), short)] * GU_PARTS
         + [pltpu.VMEM((nodes, 2 * b, LANES), short) for b in DY_BLOCKS] * 4
+        + [pltpu.VMEM((nodes // Y_LO, 2 * b, LANES), short) for b in DY_BLOCKS]
         + [pltpu.VMEM((hid, b * LANES), short) for b in DY_BLOCKS],
         compiler_params=pltpu.CompilerParams(
             collective_id=1, has_side_effects=True, vmem_limit_bytes=48 * 1024 * 1024
@@ -524,7 +588,16 @@
         name="expert_gossip",
     )(plan, *held)
 
-    return mixed_gu.reshape(width, cols), mixed_down, mean_gu, mean_down
+    results = (mixed_gu.reshape(width, cols), mixed_down, mean_gu, mean_down)
+    return pl.pallas_call(
+        put_out,
+        out_shape=tuple(jax.ShapeDtypeStruct(a.shape, a.dtype) for a in results),
+        in_specs=[pl.BlockSpec(memory_space=pltpu.VMEM)] * 4,
+        out_specs=(outside,) * 4,
+        scratch_shapes=[pltpu.SemaphoreType.DMA((4,))],
+        compiler_params=pltpu.CompilerParams(vmem_limit_bytes=1024 * 1024),
+        name="put_out",
+    )(*results)
 
 
 def solution(mesh):

time: 194 us -> 186 us (0.959)
  Pallas kernels: 189 us -> 185 us
  local copies, waits for them, and re-layouts: 4.18 us -> 0.65 us
    pallas_call x1, Pallas kernels: 189 us -> 183 us  [step(): pl.pallas_call(body, out_shape=(jax.ShapeDtypeStruct((nodes, gu_rows, col...]
    unnamed x6 -> x2, local copies, waits for them, and re-layouts: 4.18 us -> 0.65 us
where the time goes in v4:
time: 186 us
  Pallas kernels  185 us (99%)
    pallas_call x1, Pallas kernels, step(): pl.pallas_call(body, out_shape=(jax.ShapeDtypeStruct((nodes, gu_rows, col...  183 us

profile of v4, /device:TPU:1, one launch (start us, length us, event | category | flops | bytes accessed | tf_op | source)
XLA Modules:
  0.0 186.1 jit_solution(10598665043257779759)
XLA Ops:
  0.6 0.0 copy-start
  0.6 0.6 copy-done
  1.3 183.1 %expert_gossip.1 = (bf16[64,64,256]{2,1,0:T(8,128)(2,1)S(1)}, bf16[128,4096]{1,0:T(8,128)(2,1)S(1)}, f32[64,256]{1,0:T(8,128)S(1)}, f32[2,4096]{1,0:T(2,128)S(1)}) custom-call(s32[4]{0:T(128)S(1)} %copy-done, s32[2,128]{1,0:T(2,128)} %bitcast.3, bf16[128,4096]{1,0:T(8,128)(2,1)} %refs_2_.1, bf16[128,4096]{1,0:T(8,128)(2,1)} %refs_3_.1, f32[4096,256]{1,0:T(8,128)} %refs_4_.1, ...), custom_call_target="tpu_custom_call" | custom-call | tf_op jit(solution)/shard_map/expert_gossip/pallas_call | solution.py:536
  184.4 1.7 put_out.1
Async XLA Ops:
  0.6 0.7 copy-start

commit v5 on v4

--- a/solution.py
+++ b/solution.py
@@ -10,8 +10,9 @@
 MESH = pl.DeviceIdType.MESH
 ROUNDS = 4
 SHIFTS = 6
-X_PARTS = 4
-DY_BLOCKS = (4, 4, 8, 8, 8)
+X_BLOCKS = (8, 8, 8, 4, 4)
+X_PARTS = len(X_BLOCKS)
+DY_BLOCKS = (4,) * 8
 DY_PARTS = len(DY_BLOCKS)
 GU_PARTS = 4
 LANES = 128
@@ -21,7 +22,7 @@
 
 def kernel_body(
     nodes,
-    plan,
+    plan_in,
     routes,
     tokens,
     cotangent,
@@ -49,6 +50,8 @@
     mean_rows,
     mean_slab,
     mean_sem,
+    plan,
+    plan_sem,
     half_gu,
     half_down,
     send_gu,
@@ -101,10 +104,13 @@
             for base in z_bases[1:]:
                 send(base + here)
 
-    x_cols = width // X_PARTS
+    x_starts = [sum(X_BLOCKS[:c]) for c in range(X_PARTS)]
     pieces = (
         [(routes, codes, None)]
-        + [(tokens, x_all, pl.ds(c * x_cols, x_cols)) for c in range(X_PARTS)]
+        + [
+            (tokens, x_all, pl.ds(x_starts[c] * LANES, X_BLOCKS[c] * LANES))
+            for c in range(X_PARTS)
+        ]
         + [
             (cotangent, dy_all, pl.ds(starts[c] * LANES, DY_BLOCKS[c] * LANES))
             for c in range(DY_PARTS)
@@ -124,6 +130,7 @@
     loads = [
         pltpu.make_async_copy(source(p), slot(p, 0), local_sem.at[p]) for p in range(len(pieces))
     ]
+    plan_load = pltpu.make_async_copy(plan_in, plan, plan_sem)
     loads.append(pltpu.make_async_copy(param_gu, gu_wide, local_sem.at[len(pieces)]))
     home = me % plane
     along_z = [((z + d) % zs) * plane + home for d in (1, zs - 1)]
@@ -137,6 +144,7 @@
 
     for load in loads:
         load.start()
+    plan_load.start()
 
     def down_load(b):
         cols = pl.ds(pl.multiple_of(b * LANES, LANES), LANES)
@@ -176,6 +184,7 @@
         pl.semaphore_wait(enter_sem.at[r], len(others))
 
     loads[-1].wait()
+    plan_load.wait()
 
     @pl.loop(0, width // TILE)
     def _(k):
@@ -199,7 +208,7 @@
         onward[p].wait_recv()
 
     def turn(p):
-        @pl.loop(p * (x_cols // 256), (p + 1) * (x_cols // 256))
+        @pl.loop(x_starts[p] // 2, (x_starts[p] + X_BLOCKS[p]) // 2)
         def _(k):
             span = pl.ds(pl.multiple_of(k * 256, 256), 256)
             x_turned[span, :] = x_all[:, span].T
@@ -208,7 +217,7 @@
     for p in range(X_PARTS):
         arrive(1 + p)
 
-        @pl.loop(p * (x_cols // TILE), (p + 1) * (x_cols // TILE))
+        @pl.loop(x_starts[p] * LANES // TILE, (x_starts[p] + X_BLOCKS[p]) * LANES // TILE)
         def _(k):
             span = pl.ds(pl.multiple_of(k * TILE, TILE), TILE)
             both[...] += jnp.dot(
@@ -531,7 +540,7 @@
 
     held = [
         pltpu.with_memory_space_constraint(a, pltpu.HBM)
-        for a in (routes.T, tokens, cotangent, param_gu, param_down)
+        for a in (plan, routes.T, tokens, cotangent, param_gu, param_down)
     ]
     mixed_gu, mixed_down, mean_gu, mean_down = pl.pallas_call(
         body,
@@ -541,7 +550,7 @@
             jax.ShapeDtypeStruct((gu_rows, cols), wide),
             jax.ShapeDtypeStruct((hid // nodes, width), wide),
         ),
-        in_specs=[pl.BlockSpec(memory_space=pltpu.SMEM)] + [outside] * 5,
+        in_specs=[outside] * 6,
         out_specs=(everywhere,) * 4,
         scratch_shapes=[
             pltpu.VMEM((experts * rows, width), short),
@@ -562,6 +571,8 @@
             pltpu.VMEM((hid // nodes, width), wide),
             pltpu.VMEM((gu_rows, cols), wide),
             pltpu.SemaphoreType.DMA((2,)),
+            pltpu.SMEM((ROUNDS,), jnp.int32),
+            pltpu.SemaphoreType.DMA(()),
             pltpu.VMEM((nodes, gu_rows // GU_PARTS, cols), wide),
             pltpu.VMEM((nodes, down_part, LANES), wide),
             pltpu.VMEM((nodes, gu_rows, cols), short),
@@ -586,7 +597,7 @@
             collective_id=1, has_side_effects=True, vmem_limit_bytes=48 * 1024 * 1024
         ),
         name="expert_gossip",
-    )(plan, *held)
+    )(*held)
 
     results = (mixed_gu.reshape(width, cols), mixed_down, mean_gu, mean_down)
     return pl.pallas_call(

time: 186 us -> 184 us (0.989)
  Pallas kernels: 185 us -> 183 us
where the time goes in v5:
time: 184 us
  Pallas kernels  183 us (99%)
    pallas_call x1, Pallas kernels, step(): pl.pallas_call(body, out_shape=(jax.ShapeDtypeStruct((nodes, gu_rows, col...  181 us

profile of v5, /device:TPU:1, one launch (start us, length us, event | category | flops | bytes accessed | tf_op | source)
XLA Modules:
  0.0 183.8 jit_solution(4339737094597183871)
XLA Ops:
  0.6 181.4 %expert_gossip.1 = (bf16[64,64,256]{2,1,0:T(8,128)(2,1)S(1)}, bf16[128,4096]{1,0:T(8,128)(2,1)S(1)}, f32[64,256]{1,0:T(8,128)S(1)}, f32[2,4096]{1,0:T(2,128)S(1)}) custom-call(s32[4]{0:T(128)} %refs_0_.1, s32[2,128]{1,0:T(2,128)} %bitcast.3, bf16[128,4096]{1,0:T(8,128)(2,1)} %refs_2_.1, bf16[128,4096]{1,0:T(8,128)(2,1)} %refs_3_.1, f32[4096,256]{1,0:T(8,128)} %refs_4_.1, ...), custom_call_target="tpu_custom_call" | custom-call | tf_op jit(solution)/shard_map/expert_gossip/pallas_call | solution.py:545
  182.1 1.7 put_out.1

commit v6 on v5

--- a/solution.py
+++ b/solution.py
@@ -47,31 +47,27 @@
     stage,
     turned,
     mean_stage,
-    mean_rows,
-    mean_slab,
-    mean_sem,
     plan,
-    plan_sem,
     half_gu,
     half_down,
     send_gu,
     done_gu,
     enter_sem,
     local_sem,
-    block_sem,
     tok_send,
-    tok_recv,
-    gu_sem,
-    down_sem,
-    relay_sem,
-    over_sem,
-    keep_gu,
-    keep_down,
+    beside_sem,
+    across_sem,
+    onward_sem,
+    link_sem,
+    gu_in,
+    down_in,
+    relay_in,
+    home_sem,
     *landing,
 ):
     got_gu, downs = landing[:GU_PARTS], landing[GU_PARTS:]
-    send_down, got_down, done_down, home_down, relay_down, last_down = (
-        downs[i * DY_PARTS : (i + 1) * DY_PARTS] for i in range(6)
+    send_down, got_down, done_down, home_down, relay_down = (
+        downs[i * DY_PARTS : (i + 1) * DY_PARTS] for i in range(5)
     )
     me = lax.axis_index("node")
     expert = lax.axis_index("expert")
@@ -117,21 +113,31 @@
         ]
     )
 
-    def source(p):
-        src, _, cols = pieces[p]
-        return src if cols is None else src.at[:, cols]
-
     def slot(p, s):
         _, dst, cols = pieces[p]
         if cols is None:
             return dst.at[s]
         return dst.at[pl.ds(s * rows, rows), cols]
 
+    groups = [0] + [1] * X_PARTS + [2] * DY_PARTS
+
+    def held_by(g, s):
+        if g == 0:
+            return codes.at[s]
+        return (x_all, dy_all)[g - 1].at[pl.ds(s * rows, rows)]
+
     loads = [
-        pltpu.make_async_copy(source(p), slot(p, 0), local_sem.at[p]) for p in range(len(pieces))
+        pltpu.make_async_copy(src, dst, local_sem.at[g])
+        for g, (src, dst) in enumerate(
+            (
+                (routes, held_by(0, 0)),
+                (tokens, held_by(1, 0)),
+                (cotangent, held_by(2, 0)),
+                (param_gu, gu_wide),
+                (plan_in, plan),
+            )
+        )
     ]
-    plan_load = pltpu.make_async_copy(plan_in, plan, plan_sem)
-    loads.append(pltpu.make_async_copy(param_gu, gu_wide, local_sem.at[len(pieces)]))
     home = me % plane
     along_z = [((z + d) % zs) * plane + home for d in (1, zs - 1)]
     along_x = [me - x + (x + d) % X_SIZE for d in (1, X_SIZE - 1)]
@@ -144,12 +150,11 @@
 
     for load in loads:
         load.start()
-    plan_load.start()
 
     def down_load(b):
         cols = pl.ds(pl.multiple_of(b * LANES, LANES), LANES)
         dst = down_wide.at[pl.ds(pl.multiple_of(b * hid, hid), hid)]
-        return pltpu.make_async_copy(param_down.at[:, cols], dst, block_sem.at[b])
+        return pltpu.make_async_copy(param_down.at[:, cols], dst, local_sem.at[5])
 
     @pl.loop(0, width // LANES)
     def _(b):
@@ -157,23 +162,37 @@
 
     pl.semaphore_wait(barrier, 2 + len(along_z + along_x + along_y))
 
-    def token_copy(p, way, src, dst, other):
+    def token_copy(src, dst, send_sem, recv_sem, other):
         return pltpu.make_async_remote_copy(
             src_ref=src,
             dst_ref=dst,
-            send_sem=tok_send.at[way, p],
-            recv_sem=tok_recv.at[way, p],
+            send_sem=send_sem,
+            recv_sem=recv_sem,
             device_id={"expert": other},
             device_id_type=MESH,
         )
 
-    to_sibling = [token_copy(p, 0, slot(p, 0), slot(p, 1), sibling) for p in range(len(pieces))]
-    to_across = [token_copy(p, 1, slot(p, 0), slot(p, 2), across) for p in range(len(pieces))]
-    onward = [token_copy(p, 2, slot(p, 2), slot(p, 3), sibling) for p in range(len(pieces))]
+    def to_sibling(p):
+        g = groups[p]
+        return token_copy(slot(p, 0), slot(p, 1), tok_send.at[0, g], beside_sem.at[g], sibling)
+
+    def to_across(p):
+        g = groups[p]
+        return token_copy(slot(p, 0), slot(p, 2), tok_send.at[1, g], across_sem.at[p], across)
+
+    def onward(p):
+        g = groups[p]
+        return token_copy(slot(p, 2), slot(p, 3), tok_send.at[2, g], onward_sem.at[p], sibling)
+
+    def of_group(way, g):
+        every = held_by(g, 1)
+        return token_copy(every, every, tok_send.at[way, g], beside_sem.at[g], sibling)
+
     for p in range(len(pieces)):
-        loads[p].wait()
-        to_across[p].start()
-        to_sibling[p].start()
+        if groups.index(groups[p]) == p:
+            loads[groups[p]].wait()
+        to_across(p).start()
+        to_sibling(p).start()
 
     rounds = [along_z] * (zs // 2) + [along_x] * (X_SIZE // 2) + [along_y]
     for r, others in enumerate(rounds):
@@ -183,8 +202,10 @@
             )
         pl.semaphore_wait(enter_sem.at[r], len(others))
 
-    loads[-1].wait()
-    plan_load.wait()
+    loads[3].wait()
+    loads[4].wait()
+    as_rows = pl.ds(0, hid * width // param_gu.shape[1])
+    pltpu.make_async_copy(param_gu.at[as_rows], gu_wide.at[as_rows], local_sem.at[5]).wait()
 
     @pl.loop(0, width // TILE)
     def _(k):
@@ -193,7 +214,6 @@
 
     @pl.loop(0, width // LANES)
     def _(b):
-        down_load(b).wait()
         cols = pl.ds(pl.multiple_of(b * LANES, LANES), LANES)
         block = down_wide[pl.ds(pl.multiple_of(b * hid, hid), hid), :]
         down_short[:, cols] = block.astype(jnp.bfloat16)
@@ -202,10 +222,11 @@
     dact[...] = jnp.zeros_like(dact)
 
     def arrive(p):
-        to_across[p].wait_recv()
-        onward[p].start()
-        to_sibling[p].wait_recv()
-        onward[p].wait_recv()
+        to_across(p).wait_recv()
+        onward(p).start()
+        if groups.index(groups[p]) == p:
+            of_group(0, groups[p]).wait_recv()
+        onward(p).wait_recv()
 
     def turn(p):
         @pl.loop(x_starts[p] // 2, (x_starts[p] + X_BLOCKS[p]) // 2)
@@ -250,45 +271,48 @@
             preferred_element_type=jnp.float32,
         ).astype(jnp.bfloat16)
 
-    def exchange(t, src, dst, sems, c):
+    def exchange(peer, src, dst, send_sem, recv_sem):
         return pltpu.make_async_remote_copy(
             src_ref=src,
             dst_ref=dst,
-            send_sem=sems.at[0, c],
-            recv_sem=sems.at[1, c],
-            device_id={"node": t},
+            send_sem=send_sem,
+            recv_sem=recv_sem,
+            device_id={"node": peer},
             device_id_type=MESH,
         )
 
     def gu_out(peer, c):
-        return exchange(
-            peer, send_gu.at[peer, pl.ds(c * gu_part, gu_part)], got_gu[c].at[me], gu_sem, c
-        )
+        src = send_gu.at[peer, pl.ds(c * gu_part, gu_part)]
+        return exchange(peer, src, got_gu[c].at[me], link_sem.at[0], gu_in.at[c])
+
+    def some(ref, first, count, sem):
+        most = ref.at[pl.ds(first, count)]
+        return exchange((me + 1) % nodes, most, most, sem, sem)
+
+    def slices(count, values, sem):
+        return some(x_turned, 0, count * values // x_turned.shape[1], sem)
 
     spot = z * X_SIZE + x
     over = along_y[0]
 
-    def some(ref, first, count, sems, c):
-        most = ref.at[pl.ds(first, count)]
-        return exchange((me + 1) % nodes, most, most, sems, c)
-
-    def whole(got, sems, c):
-        return some(got, 0, nodes - 1, sems, c)
-
     def down_out(peer, c):
-        return exchange(peer, send_down[c].at[peer], got_down[c].at[me], down_sem, c)
+        return exchange(
+            peer, send_down[c].at[peer], got_down[c].at[me], link_sem.at[1], down_in.at[c]
+        )
 
     def down_relay(peer, c):
         other = peer - y * X_SIZE + (1 - y) * X_SIZE
-        return exchange(peer, send_down[c].at[other], relay_down[c].at[spot], relay_sem, c)
+        return exchange(
+            peer, send_down[c].at[other], relay_down[c].at[spot], link_sem.at[2], relay_in.at[c]
+        )
 
     def down_over(k, c):
         return exchange(
             over,
             relay_down[c].at[pl.ds(k * X_SIZE, X_SIZE)],
             got_down[c].at[pl.ds(k * plane + y * X_SIZE, X_SIZE)],
-            over_sem,
-            c,
+            link_sem.at[3],
+            down_in.at[c],
         )
 
     def send_row(c):
@@ -376,7 +400,7 @@
                 gu_out(peer, 0).start()
 
     for c in range(DY_PARTS):
-        some(relay_down[c], 1, nodes // Y_LO - 1, relay_sem, c).wait_recv()
+        some(relay_down[c], 1, nodes // Y_LO - 1, relay_in.at[c]).wait_recv()
 
         @pl.loop(0, zs)
         def _(k):
@@ -420,24 +444,15 @@
 
     def gu_home(peer, c):
         dst = out_gu.at[me, pl.ds(c * gu_part, gu_part)]
-        return exchange(peer, done_gu.at[c, peer], dst, gu_sem, GU_PARTS + c)
+        return exchange(peer, done_gu.at[c, peer], dst, link_sem.at[4], home_sem.at[0])
 
     def down_home(peer, c):
         return exchange(
-            peer, done_down[c].at[peer], home_down[c].at[me], down_sem, DY_PARTS + c
-        )
-
-    def put_down(c):
-        cols = pl.ds(starts[c] * LANES, DY_BLOCKS[c] * LANES)
-        return pltpu.make_async_copy(last_down[c], out_down.at[:, cols], keep_down.at[c])
-
-    def own_gu(c):
-        dst = out_gu.at[me, pl.ds(c * gu_part, gu_part)]
-        return pltpu.make_async_copy(done_gu.at[c, me], dst, keep_gu.at[c])
+            peer, done_down[c].at[peer], home_down[c].at[me], link_sem.at[5], home_sem.at[1]
+        )
 
     for c in range(DY_PARTS):
-        some(got_down[c], 0, nodes // Y_LO - 1, down_sem, c).wait_recv()
-        some(got_down[c], 0, nodes // Y_LO, over_sem, c).wait_recv()
+        some(got_down[c], 0, nodes - 1, down_in.at[c]).wait_recv()
         blocks = DY_BLOCKS[c]
         filtered(
             got_down[c],
@@ -448,7 +463,7 @@
         for r in range(2):
             for i in range(blocks):
                 at = (starts[c] + i) * LANES
-                mean_rows[r : r + 1, at : at + LANES] = mean_stage[
+                mean_down[r : r + 1, at : at + LANES] = mean_stage[
                     r * blocks + i : r * blocks + i + 1, :
                 ]
 
@@ -457,24 +472,19 @@
         home_down[c][me] = done_down[c][me]
 
     for c in range(GU_PARTS):
-        whole(got_gu[c], gu_sem, c).wait_recv()
+        some(got_gu[c], 0, nodes - 1, gu_in.at[c]).wait_recv()
         filtered(
-            got_gu[c], half_gu, done_gu.at[c], mean_slab.at[pl.ds(c * gu_part, gu_part)]
+            got_gu[c], half_gu, done_gu.at[c], mean_gu.at[pl.ds(c * gu_part, gu_part)]
         )
 
         each_peer(lambda peer: gu_home(peer, c).start())
 
-        own_gu(c).start()
-
-    means = [
-        pltpu.make_async_copy(mean_slab, mean_gu, mean_sem.at[0]),
-        pltpu.make_async_copy(mean_rows, mean_down, mean_sem.at[1]),
-    ]
-    for copy in means:
-        copy.start()
+        out_gu[me, pl.ds(c * gu_part, gu_part)] = done_gu[c, me]
+
+    gu_values, down_values = gu_rows * param_gu.shape[1], hid // nodes * width
+    slices(nodes - 1, down_values, home_sem.at[1]).wait_recv()
 
     for c in range(DY_PARTS):
-        whole(got_down[c], down_sem, DY_PARTS + c).wait_recv()
         blocks = DY_BLOCKS[c]
         down_part = 2 * blocks
 
@@ -489,33 +499,33 @@
                 turned[pl.ds(i * hid + r, nodes, stride=2), :] = stage[
                     pl.ds(row, nodes, stride=down_part), :
                 ]
-            last_down[c][:, i * LANES : (i + 1) * LANES] = turned[
+            at = (starts[c] + i) * LANES
+            out_down[:, at : at + LANES] = turned[
                 i * hid : (i + 1) * hid, :
             ].astype(jnp.bfloat16)
-        put_down(c).start()
-
-    for copy in means:
-        copy.wait()
-    for p in range(len(pieces)):
-        to_sibling[p].wait_send()
-        to_across[p].wait_send()
-        onward[p].wait_send()
-    for c in range(DY_PARTS):
-        some(got_down[c], 0, nodes // Y_LO - 1, down_sem, c).wait_send()
-        some(relay_down[c], 1, nodes // Y_LO - 1, relay_sem, c).wait_send()
-        some(got_down[c], 0, nodes // Y_LO, over_sem, c).wait_send()
-        whole(got_down[c], down_sem, DY_PARTS + c).wait_send()
-        put_down(c).wait()
-    for c in range(GU_PARTS):
-        whole(got_gu[c], gu_sem, c).wait_send()
-        whole(got_gu[c], gu_sem, GU_PARTS + c).wait_send()
-        whole(got_gu[c], gu_sem, GU_PARTS + c).wait_recv()
-        own_gu(c).wait()
+
+    for g in range(3):
+        for way in range(3):
+            of_group(way, g).wait_send()
+    slices(nodes - 1, gu_values, link_sem.at[0]).wait_send()
+    slices(nodes // Y_LO - 1, down_values, link_sem.at[1]).wait_send()
+    slices(nodes // Y_LO - 1, down_values, link_sem.at[2]).wait_send()
+    slices(nodes // Y_LO, down_values, link_sem.at[3]).wait_send()
+    slices(nodes - 1, gu_values, link_sem.at[4]).wait_send()
+    slices(nodes - 1, down_values, link_sem.at[5]).wait_send()
+    slices(nodes - 1, gu_values, home_sem.at[0]).wait_recv()
 
 
 def put_out(*refs):
-    sems = refs[-1]
-    copies = [pltpu.make_async_copy(refs[i], refs[4 + i], sems.at[i]) for i in range(4)]
+    sems, copies = refs[-1], []
+    for i in range(4):
+        pieces = 4 if refs[i].shape[0] % 64 == 0 else 1
+        share = refs[i].shape[0] // pieces
+        for k in range(pieces):
+            span = pl.ds(k * share, share)
+            copies.append(
+                pltpu.make_async_copy(refs[i].at[span], refs[4 + i].at[span], sems.at[len(copies)])
+            )
     for copy in copies:
         copy.start()
     for copy in copies:
@@ -531,7 +541,7 @@
     gu_rows = width // nodes
     down_part = 2 * max(DY_BLOCKS)
     pieces = X_PARTS + 1 + DY_PARTS
-    everywhere = pl.BlockSpec(memory_space=pl.ANY)
+    inside = pl.BlockSpec(memory_space=pltpu.VMEM)
     outside = pl.BlockSpec(memory_space=pltpu.HBM)
     short, wide = jnp.bfloat16, jnp.float32
 
@@ -551,7 +561,7 @@
             jax.ShapeDtypeStruct((hid // nodes, width), wide),
         ),
         in_specs=[outside] * 6,
-        out_specs=(everywhere,) * 4,
+        out_specs=(inside,) * 4,
         scratch_shapes=[
             pltpu.VMEM((experts * rows, width), short),
             pltpu.VMEM((experts * rows, width), short),
@@ -568,31 +578,26 @@
             pltpu.VMEM((nodes * down_part, LANES), wide),
             pltpu.VMEM((nodes * down_part, LANES), wide),
             pltpu.VMEM((down_part, LANES), wide),
-            pltpu.VMEM((hid // nodes, width), wide),
-            pltpu.VMEM((gu_rows, cols), wide),
-            pltpu.SemaphoreType.DMA((2,)),
             pltpu.SMEM((ROUNDS,), jnp.int32),
-            pltpu.SemaphoreType.DMA(()),
             pltpu.VMEM((nodes, gu_rows // GU_PARTS, cols), wide),
             pltpu.VMEM((nodes, down_part, LANES), wide),
             pltpu.VMEM((nodes, gu_rows, cols), short),
             pltpu.VMEM((GU_PARTS, nodes, gu_rows // GU_PARTS, cols), short),
             pltpu.SemaphoreType.REGULAR((nodes // (Y_LO * X_SIZE) // 2 + X_SIZE // 2 + 1,)),
-            pltpu.SemaphoreType.DMA((1 + pieces,)),
-            pltpu.SemaphoreType.DMA((width // LANES,)),
-            pltpu.SemaphoreType.DMA((3, pieces)),
-            pltpu.SemaphoreType.DMA((3, pieces)),
-            pltpu.SemaphoreType.DMA((2, 2 * GU_PARTS)),
-            pltpu.SemaphoreType.DMA((2, 2 * DY_PARTS)),
-            pltpu.SemaphoreType.DMA((2, DY_PARTS)),
-            pltpu.SemaphoreType.DMA((2, DY_PARTS)),
+            pltpu.SemaphoreType.DMA((6,)),
+            pltpu.SemaphoreType.DMA((3, 3)),
+            pltpu.SemaphoreType.DMA((3,)),
+            pltpu.SemaphoreType.DMA((pieces,)),
+            pltpu.SemaphoreType.DMA((pieces,)),
+            pltpu.SemaphoreType.DMA((6,)),
             pltpu.SemaphoreType.DMA((GU_PARTS,)),
             pltpu.SemaphoreType.DMA((DY_PARTS,)),
+            pltpu.SemaphoreType.DMA((DY_PARTS,)),
+            pltpu.SemaphoreType.DMA((2,)),
         ]
         + [pltpu.VMEM((nodes, gu_rows // GU_PARTS, cols), short)] * GU_PARTS
         + [pltpu.VMEM((nodes, 2 * b, LANES), short) for b in DY_BLOCKS] * 4
-        + [pltpu.VMEM((nodes // Y_LO, 2 * b, LANES), short) for b in DY_BLOCKS]
-        + [pltpu.VMEM((hid, b * LANES), short) for b in DY_BLOCKS],
+        + [pltpu.VMEM((nodes // Y_LO, 2 * b, LANES), short) for b in DY_BLOCKS],
         compiler_params=pltpu.CompilerParams(
             collective_id=1, has_side_effects=True, vmem_limit_bytes=48 * 1024 * 1024
         ),
@@ -603,9 +608,9 @@
     return pl.pallas_call(
         put_out,
         out_shape=tuple(jax.ShapeDtypeStruct(a.shape, a.dtype) for a in results),
-        in_specs=[pl.BlockSpec(memory_space=pltpu.VMEM)] * 4,
+        in_specs=[inside] * 4,
         out_specs=(outside,) * 4,
-        scratch_shapes=[pltpu.SemaphoreType.DMA((4,))],
+        scratch_shapes=[pltpu.SemaphoreType.DMA((13,))],
         compiler_params=pltpu.CompilerParams(vmem_limit_bytes=1024 * 1024),
         name="put_out",
     )(*results)

time: 184 us -> 183 us (level)
  no operation moved by 1% of the time
where the time goes in v6:
time: 183 us; the launch traced here: 182 us
  Pallas kernels  182 us (99%)
    pallas_call x1, Pallas kernels, step(): pl.pallas_call(body, out_shape=(jax.ShapeDtypeStruct((nodes, gu_rows, col...  180 us

profile of v6, /device:TPU:1, one launch (start us, length us, event | category | flops | bytes accessed | tf_op | source)
XLA Modules:
  0.0 182.5 jit_solution(7871933750944070496)
XLA Ops:
  0.6 180.1 %expert_gossip.1 = (bf16[64,64,256]{2,1,0:T(8,128)(2,1)S(1)}, bf16[128,4096]{1,0:T(8,128)(2,1)S(1)}, f32[64,256]{1,0:T(8,128)S(1)}, f32[2,4096]{1,0:T(2,128)S(1)}) custom-call(s32[4]{0:T(128)} %refs_0_.1, s32[2,128]{1,0:T(2,128)} %bitcast.3, bf16[128,4096]{1,0:T(8,128)(2,1)} %refs_2_.1, bf16[128,4096]{1,0:T(8,128)(2,1)} %refs_3_.1, f32[4096,256]{1,0:T(8,128)} %refs_4_.1, ...), custom_call_target="tpu_custom_call" | custom-call | tf_op jit(solution)/shard_map/expert_gossip/pallas_call | solution.py:555
  180.7 1.8 put_out.1

commit v7 on v6

--- a/solution.py
+++ b/solution.py
@@ -83,7 +83,7 @@
     gu_part = gu_rows // GU_PARTS
     starts = [sum(DY_BLOCKS[:c]) for c in range(DY_PARTS)]
 
-    steps = [0] + [d for j in range(1, zs // 2) for d in (j, zs - j)] + [zs // 2]
+    steps = [0, zs // 2] + [d for j in range(zs // 2 - 1, 0, -1) for d in (j, zs - j)]
     z_bases = [((z + d) % zs) * plane for d in steps]
 
     def in_plane(k):
@@ -355,10 +355,12 @@
                     row = r * blocks + k * (TILE // LANES) + i
                     stage[pl.ds(row, nodes, stride=down_part), :] = new
 
-        @pl.loop(0, nodes)
-        def _(n):
-            span = pl.ds(pl.multiple_of(n * down_part, down_part), down_part)
-            send_down[c][n] = stage[span, :].astype(jnp.bfloat16)
+        some_nodes = 16
+        for n in range(0, nodes, some_nodes):
+            block = stage[n * down_part : (n + some_nodes) * down_part, :]
+            send_down[c][n : n + some_nodes] = block.reshape(
+                some_nodes, down_part, LANES
+            ).astype(jnp.bfloat16)
 
         send_row(c)
         got_down[c][me] = send_down[c][me]
@@ -380,7 +382,7 @@
 
     @pl.loop(0, zs)
     def _(j):
-        zt = (z + (j % 2) * ((j + 1) // 2) + (1 - j % 2) * (zs - j // 2)) % zs
+        zt = (z + zs // 2 + (1 - j % 2) * (j // 2) - (j % 2) * ((j + 1) // 2)) % zs
         at = pl.multiple_of(zt * (plane * gu_rows), plane * gu_rows)
         span = pl.ds(at, plane * gu_rows)
         grad = jnp.dot(x_turned[span, :], dboth[...], preferred_element_type=jnp.float32)
@@ -392,7 +394,7 @@
             peer = zt * plane + in_plane(k)
             if k == 0:
 
-                @pl.when(j > 0)
+                @pl.when(j < zs - 1)
                 def _():
                     gu_out(peer, 0).start()
 

time: 183 us -> 181 us (0.989)
  Pallas kernels: 182 us -> 180 us
where the time goes in v7:
time: 181 us
  Pallas kernels  180 us (99%)
    pallas_call x1, Pallas kernels, step(): pl.pallas_call(body, out_shape=(jax.ShapeDtypeStruct((nodes, gu_rows, col...  179 us

profile of v7, /device:TPU:1, one launch (start us, length us, event | category | flops | bytes accessed | tf_op | source)
XLA Modules:
  0.0 181.0 jit_solution(8618094193500444546)
XLA Ops:
  0.6 178.6 %expert_gossip.1 = (bf16[64,64,256]{2,1,0:T(8,128)(2,1)S(1)}, bf16[128,4096]{1,0:T(8,128)(2,1)S(1)}, f32[64,256]{1,0:T(8,128)S(1)}, f32[2,4096]{1,0:T(2,128)S(1)}) custom-call(s32[4]{0:T(128)} %refs_0_.1, s32[2,128]{1,0:T(2,128)} %bitcast.3, bf16[128,4096]{1,0:T(8,128)(2,1)} %refs_2_.1, bf16[128,4096]{1,0:T(8,128)(2,1)} %refs_3_.1, f32[4096,256]{1,0:T(8,128)} %refs_4_.1, ...), custom_call_target="tpu_custom_call" | custom-call | tf_op jit(solution)/shard_map/expert_gossip/pallas_call | solution.py:557
  179.2 1.8 put_out.1

commit v8 on v7

--- a/solution.py
+++ b/solution.py
@@ -330,21 +330,28 @@
             for base in z_bases[1:]:
                 both_ways(base + here)
 
-    for c in range(DY_PARTS):
-        arrive(1 + X_PARTS + c)
-        blocks = DY_BLOCKS[c]
-        down_part = 2 * blocks
-
-        @pl.loop(0, blocks * LANES // TILE)
-        def _(k):
-            at = pl.multiple_of(starts[c] * LANES + k * TILE, TILE)
-            span = pl.ds(at, TILE)
+    def add_dact(c):
+        @pl.loop(0, DY_BLOCKS[c] * LANES // TILE)
+        def _(k):
+            span = pl.ds(pl.multiple_of(starts[c] * LANES + k * TILE, TILE), TILE)
             dact[...] += lax.dot_general(
                 dy_all[:, span],
                 down_short[:, span],
                 (((1,), (1,)), ((), ())),
                 preferred_element_type=jnp.float32,
             )
+
+    for c in range(DY_PARTS):
+        arrive(1 + X_PARTS + c)
+        if c == DY_PARTS - 1:
+            add_dact(c)
+        blocks = DY_BLOCKS[c]
+        down_part = 2 * blocks
+
+        @pl.loop(0, blocks * LANES // TILE)
+        def _(k):
+            at = pl.multiple_of(starts[c] * LANES + k * TILE, TILE)
+            span = pl.ds(at, TILE)
             grad = jnp.dot(act_turned[...], dy_all[:, span], preferred_element_type=jnp.float32)
             grad = grad * (0.5 * hid_scale)
             for r in range(2):
@@ -363,6 +370,8 @@
             ).astype(jnp.bfloat16)
 
         send_row(c)
+        if c < DY_PARTS - 1:
+            add_dact(c)
         got_down[c][me] = send_down[c][me]
         relay_down[c][spot] = send_down[c][over]
         if c == 1:

time: 181 us -> 181 us (level)
  no operation moved by 1% of the time
where the time goes in v8:
time: 181 us
  Pallas kernels  180 us (99%)
    pallas_call x1, Pallas kernels, step(): pl.pallas_call(body, out_shape=(jax.ShapeDtypeStruct((nodes, gu_rows, col...  179 us

profile of v8, /device:TPU:1, one launch (start us, length us, event | category | flops | bytes accessed | tf_op | source)
XLA Modules:
  0.0 181.0 jit_solution(14077550864759023087)
XLA Ops:
  0.6 178.5 %expert_gossip.1 = (bf16[64,64,256]{2,1,0:T(8,128)(2,1)S(1)}, bf16[128,4096]{1,0:T(8,128)(2,1)S(1)}, f32[64,256]{1,0:T(8,128)S(1)}, f32[2,4096]{1,0:T(2,128)S(1)}) custom-call(s32[4]{0:T(128)} %refs_0_.1, s32[2,128]{1,0:T(2,128)} %bitcast.3, bf16[128,4096]{1,0:T(8,128)(2,1)} %refs_2_.1, bf16[128,4096]{1,0:T(8,128)(2,1)} %refs_3_.1, f32[4096,256]{1,0:T(8,128)} %refs_4_.1, ...), custom_call_target="tpu_custom_call" | custom-call | tf_op jit(solution)/shard_map/expert_gossip/pallas_call | solution.py:566
  179.2 1.8 put_out.1
